TPU v7x, 128 devices: a whole 4x4x4 slice. The times are simulated.
128 devices in a mesh: dp: 32 (over y, z, core), mp: 4 (over x).
Axes of the slice: x: 4, y: 4, z: 4, core: 2. Of those that a mesh axis runs over, the one named last changes fastest.
Arguments:
- table: float32 [262144, 512], P('dp', 'mp'), may hold values from -6 to 6
- first_moment: float32 [262144, 512], P('dp', 'mp'), may hold values from -1.8 to 1.8
- second_moment: float32 [262144, 512], P('dp', 'mp'), may hold values from 0.01 to 1
- grads: bfloat16 [65536, 512], P('dp', 'mp'), may hold values from -108 to 108
- ids: int32 [65536], P('dp'), may hold values from 0 to 262143, as said below
Outputs:
- new_table: float32 [262144, 512], P('dp', 'mp')
- new_first: float32 [262144, 512], P('dp', 'mp')
- new_second: float32 [262144, 512], P('dp', 'mp')
Inputs may be any that keep to these rules, and one draw needn't show every extreme that they name: `ids`: the positions of one device name at most 256 positions' worth of rows of any one owner (rows k * 8192 to (k + 1) * 8192 - 1) and at most 64 distinct rows of one owner; in every draw one owner reaches both bounds on every device.
All inputs are finite; a program needn't handle non-finite values.
Results may differ from a plain program's by a relative error of at most 0.0003.
Values may be sent and summed in bfloat16 or wider, within the bound.
A program may use at most 64 MiB of HBM per device.

v0:
```python
import jax
import jax.numpy as jnp
from jax import lax
from jax.sharding import Mesh
from jax.sharding import PartitionSpec as P

DP = ("dp_0", "dp_1", "dp_2")
DP_MP = ("dp_0", "dp_1", "dp_2", "mp")


beta_first = 0.9
beta_second = 0.999
learn_rate = 0.01
decay_rate = 0.1
adam_eps = 1e-08
first_fix = 0.9999734386
second_fix = 0.0952078529


def by_axis(shard, axes):
    for axis in axes:
        shard = lax.psum(shard, axis)
    return shard


def block_size():
    return 512


def block_starts(count, step):
    return jnp.arange(0, count, step, dtype=jnp.int32)


def pack_slots(dest, local_row, values, slots, rows_dev):
    step = block_size()

    def pack_one_block(start):
        target = start + jnp.arange(step, dtype=jnp.int32)
        match = dest[None, :] == target[:, None]
        summed = jnp.dot(match.astype(jnp.bfloat16), values, preferred_element_type=jnp.float32)
        marks = jnp.min(jnp.where(match, local_row[None, :], rows_dev), axis=1)
        return (summed, marks)

    summed, marks = lax.map(pack_one_block, block_starts(slots, step))
    return (summed.reshape(slots, values.shape[1]), marks.reshape(slots))


def gather_rows(got_row, got, rows_dev):
    step = block_size()

    def gather_one_block(start):
        target = start + jnp.arange(step, dtype=jnp.int32)
        match = got_row[None, :] == target[:, None]
        return jnp.dot(
            match.astype(jnp.float32),
            got,
            precision=lax.Precision.HIGHEST,
            preferred_element_type=jnp.float32,
        )

    return lax.map(gather_one_block, block_starts(rows_dev, step)).reshape(rows_dev, got.shape[1])


def body(table, first_moment, second_moment, grads, ids):
    peers = lax.axis_size(DP)
    rows_dev = table.shape[0]
    width = table.shape[1]
    tok_dev = grads.shape[0]
    room = tok_dev // peers
    owner = ids // rows_dev
    local_row = ids - owner * rows_dev
    place = jnp.arange(tok_dev, dtype=jnp.int32)
    step = block_size()

    def first_block(start):
        here = start + jnp.arange(step, dtype=jnp.int32)
        mine = lax.dynamic_slice_in_dim(ids, start, step)
        earlier = jnp.logical_and(ids[None, :] == mine[:, None], place[None, :] < here[:, None])
        return jnp.logical_not(jnp.any(earlier, axis=1))

    leading = lax.map(first_block, block_starts(tok_dev, step)).reshape(tok_dev)

    def rank_block(start):
        mine = lax.dynamic_slice_in_dim(ids, start, step)
        mine_owner = lax.dynamic_slice_in_dim(owner, start, step)
        below = (
            leading[None, :]
            & (owner[None, :] == mine_owner[:, None])
            & (ids[None, :] < mine[:, None])
        )
        return jnp.sum(below.astype(jnp.int32), axis=1)

    rank = lax.map(rank_block, block_starts(tok_dev, step)).reshape(tok_dev)
    dest = owner * room + rank
    slots = peers * room
    sums, marker = pack_slots(dest, local_row, grads, slots, rows_dev)
    row_marks = marker.astype(jnp.float32).reshape(peers, room)
    got, got_rows = (
        lax.all_to_all(
            sums.reshape(peers, room, width), DP, split_axis=0, concat_axis=0, tiled=True
        ),
        lax.all_to_all(row_marks, DP, split_axis=0, concat_axis=0, tiled=True),
    )
    got_index = got_rows.reshape(slots).astype(jnp.int32)
    grad_rows = gather_rows(got_index, got.reshape(slots, width), rows_dev)
    local_sum = jnp.sum(grad_rows * grad_rows)
    total = by_axis(local_sum, DP_MP)
    limit = jnp.sqrt(jnp.float32(tok_dev * peers * width * lax.axis_size("mp")))
    scale = limit / jnp.maximum(jnp.sqrt(total), limit)
    clipped = scale * grad_rows
    new_first = beta_first * first_moment + (1.0 - beta_first) * clipped
    new_second = beta_second * second_moment + (1.0 - beta_second) * clipped * clipped
    first_hat = new_first / first_fix
    second_hat = new_second / second_fix
    new_table = table - learn_rate * (
        first_hat / (jnp.sqrt(second_hat) + adam_eps) + decay_rate * table
    )
    return (new_table, new_first, new_second)


def solution(mesh):
    split = Mesh(mesh.devices.reshape(4, 4, 2, mesh.shape["mp"]), ("dp_0", "dp_1", "dp_2", "mp"))
    placed = (P(DP, "mp"), P(DP, "mp"), P(DP, "mp"), P(DP, "mp"), P(DP))
    return jax.shard_map(
        body,
        mesh=split,
        in_specs=placed,
        out_specs=(P(DP, "mp"), P(DP, "mp"), P(DP, "mp")),
        check_vma=False,
    )
```

profile of v0, /device:TPU:1, one launch (start us, length us, event | category | flops | bytes accessed | tf_op | source)
XLA Modules:
  0.0 211.3 jit_solution(10993238454056998572)
XLA Ops:
  1.4 22.3 %while.46 = (s32[]{:T(128)}, pred[4,512]{1,0:T(4,128)(4,1)S(1)}, s32[2048]{0:T(1024)}, s32[4]{0:T(128)S(1)}, s32[]{:T(128)}, /*index=5*/s32[]{:T(128)}, s32[]{:T(128)}) while((s32[]{:T(128)}, pred[4,512]{1,0:T(4,128)(4,1)S(1)}, s32[2048]{0:T(1024)}, s32[4]{0:T(128)S(1)}, s32[]{:T(128)}, /*index=5*/s32[]{:T(128)}, s32[]{:T(128)}) %tuple.67), condition=%wide.region_2.3_spmd.clone, body=%wide.region_0.2_spmd.clone.sunk | while | flops 4194821 | bytes 22159 | solution.py:81
  23.7 20.1 %while.43 = (s32[]{:T(128)}, s32[4,512]{1,0:T(4,128)S(1)}, pred[4,512]{1,0:T(4,128)(4,1)S(1)}, s32[2048]{0:T(1024)S(1)}, s32[4]{0:T(128)S(1)}, /*index=5*/s32[2048]{0:T(1024)}, s32[]{:T(128)}, s32[]{:T(128)}, s32[]{:T(128)}) while((s32[]{:T(128)}, s32[4,512]{1,0:T(4,128)S(1)}, pred[4,512]{1,0:T(4,128)(4,1)S(1)}, s32[2048]{0:T(1024)S(1)}, ...), condition=%wide.region_5.6_spmd, body=%wide.region_3.5_spmd.sunk | while | flops 6290949 | bytes 41119 | solution.py:93
  44.5 18.4 %while.44 = (s32[]{:T(128)}, f32[4,512,128]{2,1,0:T(8,128)}, s32[4,512]{1,0:T(4,128)S(1)}, s32[2048]{0:T(1024)S(1)}, s32[4]{0:T(128)S(1)}, /*index=5*/bf16[2048,...) while((s32[]{:T(128)}, f32[4,512,128]{2,1,0:T(8,128)}, s32[4,512]{1,0:T(4,128)S(1)}, ...), condition=%wide.region_8.9_spmd, body=%wide.region_6.8_spmd.sunk | while | flops 272629760 | bytes 823421 | solution.py:44
  46.6 2.5 %fusion.43 = f32[4,512,128]{2,1,0:T(8,128)} fusion(f32[4,512,128]{2,1,0:T(8,128)} %get-tuple-element.385, s32[]{:T(128)S(6)} %copy.32, bf16[2048,128]{1,0:T(8,128)(2,1)} %get-tuple-element.398, s32[2048]{0:T(1024)S(1)} %get-tuple-element.396, s32[512]{0:T(512)S(1)} %iota_add_fusion.6), kind=kOutput, calls=%fused_computation.9.clone.1 | convolution fusion | flops 269484032 | bytes 796676 | tf_op jit(solution)/shard_map/while/body/eval_jaxpr/dot_general | solution.py:40
  60.4 2.5 %fusion.43 = f32[4,512,128]{2,1,0:T(8,128)} fusion(f32[4,512,128]{2,1,0:T(8,128)} %get-tuple-element.385, s32[]{:T(128)S(6)} %copy.32, bf16[2048,128]{1,0:T(8,128)(2,1)} %get-tuple-element.398, s32[2048]{0:T(1024)S(1)} %get-tuple-element.396, s32[512]{0:T(512)S(1)} %iota_add_fusion.6), kind=kOutput, calls=%fused_computation.9.clone.1 | convolution fusion | flops 269484032 | bytes 796676 | tf_op jit(solution)/shard_map/while/body/eval_jaxpr/dot_general | solution.py:40
  63.0 16.4 %all_to_all.11 = f32[32,1,64]{2,1,0:T(1,128)S(1)} all-to-all(f32[32,1,64]{2,1,0:T(1,128)S(1)} %convert_element_type.26), channel_id=1, replica_groups=mesh['dp_0'=4,'dp_1'=4,'dp_2'=2,'mp'=4] {'dp_0','dp_1','dp_2'}, dimensions={0} | all-to-all | bytes 16384 | tf_op jit(solution)/shard_map/all_to_all | solution.py:102
  79.4 4.2 %all-to-all-start.1 = ((f32[32,64,128]{2,1,0:T(8,128)}), f32[32,64,128]{2,1,0:T(8,128)S(1)}, u32[]{:S(2)}, u32[]{:S(2)}) async-start(f32[32,64,128]{2,1,0:T(8,128)} %bitcast.7), calls=%async_computation.1 | async-start | bytes 2097152 | tf_op jit(solution)/shard_map/all_to_all | solution.py:99
  83.8 16.9 %all-to-all-done.1 = f32[32,64,128]{2,1,0:T(8,128)S(1)} async-done(((f32[32,64,128]{2,1,0:T(8,128)}), f32[32,64,128]{2,1,0:T(8,128)S(1)}, u32[]{:S(2)}, u32[]{:S(2)}) %all-to-all-start.1) | async-done | bytes 1048608 | tf_op jit(solution)/shard_map/all_to_all | solution.py:99
  100.7 62.8 %while.45 = (s32[]{:T(128)}, f32[16,512,128]{2,1,0:T(8,128)}, s32[2048]{0:T(1024)S(1)}, s32[16]{0:T(128)S(1)}, f32[2048,128]{1,0:T(8,128)S(1)}, /*index=5*/s32[]{:T(128)}) while((s32[]{:T(128)}, f32[16,512,128]{2,1,0:T(8,128)}, s32[2048]{0:T(1024)S(1)}, s32[16]{0:T(128)S(1)}, f32[2048,128]{1,0:T(8,128)S(1)}, /*index=5*/s32[]{:T(128)}) %tuple.79), condition=%wide.region_10.11_spmd, body=%wide.region_9.10_spmd.sunk | while | flops 1611661824 | bytes 1323105 | solution.py:61
  101.9 2.7 %fusion.47 = f32[16,512,128]{2,1,0:T(8,128)} fusion(f32[16,512,128]{2,1,0:T(8,128)} %get-tuple-element.409, s32[]{:T(128)S(6)} %copy.40, f32[2048,128]{1,0:T(8,128)S(1)} %get-tuple-element.418, s32[2048]{0:T(1024)S(1)} %get-tuple-element.416, s32[512]{0:T(512)S(1)} %iota_add_fusion.7), kind=kOutput, calls=%fused_computation.16.clone.1 | convolution fusion | flops 1611661312 | bytes 1320964 | tf_op jit(solution)/shard_map/while/body/eval_jaxpr/dot_general | solution.py:54
  105.8 2.7 %fusion.47 = f32[16,512,128]{2,1,0:T(8,128)} fusion(f32[16,512,128]{2,1,0:T(8,128)} %get-tuple-element.409, s32[]{:T(128)S(6)} %copy.40, f32[2048,128]{1,0:T(8,128)S(1)} %get-tuple-element.418, s32[2048]{0:T(1024)S(1)} %get-tuple-element.416, s32[512]{0:T(512)S(1)} %iota_add_fusion.7), kind=kOutput, calls=%fused_computation.16.clone.1 | convolution fusion | flops 1611661312 | bytes 1320964 | tf_op jit(solution)/shard_map/while/body/eval_jaxpr/dot_general | solution.py:54
  109.7 2.7 %fusion.47 = f32[16,512,128]{2,1,0:T(8,128)} fusion(f32[16,512,128]{2,1,0:T(8,128)} %get-tuple-element.409, s32[]{:T(128)S(6)} %copy.40, f32[2048,128]{1,0:T(8,128)S(1)} %get-tuple-element.418, s32[2048]{0:T(1024)S(1)} %get-tuple-element.416, s32[512]{0:T(512)S(1)} %iota_add_fusion.7), kind=kOutput, calls=%fused_computation.16.clone.1 | convolution fusion | flops 1611661312 | bytes 1320964 | tf_op jit(solution)/shard_map/while/body/eval_jaxpr/dot_general | solution.py:54
  113.7 2.7 %fusion.47 = f32[16,512,128]{2,1,0:T(8,128)} fusion(f32[16,512,128]{2,1,0:T(8,128)} %get-tuple-element.409, s32[]{:T(128)S(6)} %copy.40, f32[2048,128]{1,0:T(8,128)S(1)} %get-tuple-element.418, s32[2048]{0:T(1024)S(1)} %get-tuple-element.416, s32[512]{0:T(512)S(1)} %iota_add_fusion.7), kind=kOutput, calls=%fused_computation.16.clone.1 | convolution fusion | flops 1611661312 | bytes 1320964 | tf_op jit(solution)/shard_map/while/body/eval_jaxpr/dot_general | solution.py:54
  117.6 2.7 %fusion.47 = f32[16,512,128]{2,1,0:T(8,128)} fusion(f32[16,512,128]{2,1,0:T(8,128)} %get-tuple-element.409, s32[]{:T(128)S(6)} %copy.40, f32[2048,128]{1,0:T(8,128)S(1)} %get-tuple-element.418, s32[2048]{0:T(1024)S(1)} %get-tuple-element.416, s32[512]{0:T(512)S(1)} %iota_add_fusion.7), kind=kOutput, calls=%fused_computation.16.clone.1 | convolution fusion | flops 1611661312 | bytes 1320964 | tf_op jit(solution)/shard_map/while/body/eval_jaxpr/dot_general | solution.py:54
  121.5 2.7 %fusion.47 = f32[16,512,128]{2,1,0:T(8,128)} fusion(f32[16,512,128]{2,1,0:T(8,128)} %get-tuple-element.409, s32[]{:T(128)S(6)} %copy.40, f32[2048,128]{1,0:T(8,128)S(1)} %get-tuple-element.418, s32[2048]{0:T(1024)S(1)} %get-tuple-element.416, s32[512]{0:T(512)S(1)} %iota_add_fusion.7), kind=kOutput, calls=%fused_computation.16.clone.1 | convolution fusion | flops 1611661312 | bytes 1320964 | tf_op jit(solution)/shard_map/while/body/eval_jaxpr/dot_general | solution.py:54
  125.4 2.7 %fusion.47 = f32[16,512,128]{2,1,0:T(8,128)} fusion(f32[16,512,128]{2,1,0:T(8,128)} %get-tuple-element.409, s32[]{:T(128)S(6)} %copy.40, f32[2048,128]{1,0:T(8,128)S(1)} %get-tuple-element.418, s32[2048]{0:T(1024)S(1)} %get-tuple-element.416, s32[512]{0:T(512)S(1)} %iota_add_fusion.7), kind=kOutput, calls=%fused_computation.16.clone.1 | convolution fusion | flops 1611661312 | bytes 1320964 | tf_op jit(solution)/shard_map/while/body/eval_jaxpr/dot_general | solution.py:54
  129.3 2.7 %fusion.47 = f32[16,512,128]{2,1,0:T(8,128)} fusion(f32[16,512,128]{2,1,0:T(8,128)} %get-tuple-element.409, s32[]{:T(128)S(6)} %copy.40, f32[2048,128]{1,0:T(8,128)S(1)} %get-tuple-element.418, s32[2048]{0:T(1024)S(1)} %get-tuple-element.416, s32[512]{0:T(512)S(1)} %iota_add_fusion.7), kind=kOutput, calls=%fused_computation.16.clone.1 | convolution fusion | flops 1611661312 | bytes 1320964 | tf_op jit(solution)/shard_map/while/body/eval_jaxpr/dot_general | solution.py:54
  133.3 2.7 %fusion.47 = f32[16,512,128]{2,1,0:T(8,128)} fusion(f32[16,512,128]{2,1,0:T(8,128)} %get-tuple-element.409, s32[]{:T(128)S(6)} %copy.40, f32[2048,128]{1,0:T(8,128)S(1)} %get-tuple-element.418, s32[2048]{0:T(1024)S(1)} %get-tuple-element.416, s32[512]{0:T(512)S(1)} %iota_add_fusion.7), kind=kOutput, calls=%fused_computation.16.clone.1 | convolution fusion | flops 1611661312 | bytes 1320964 | tf_op jit(solution)/shard_map/while/body/eval_jaxpr/dot_general | solution.py:54
  137.2 2.7 %fusion.47 = f32[16,512,128]{2,1,0:T(8,128)} fusion(f32[16,512,128]{2,1,0:T(8,128)} %get-tuple-element.409, s32[]{:T(128)S(6)} %copy.40, f32[2048,128]{1,0:T(8,128)S(1)} %get-tuple-element.418, s32[2048]{0:T(1024)S(1)} %get-tuple-element.416, s32[512]{0:T(512)S(1)} %iota_add_fusion.7), kind=kOutput, calls=%fused_computation.16.clone.1 | convolution fusion | flops 1611661312 | bytes 1320964 | tf_op jit(solution)/shard_map/while/body/eval_jaxpr/dot_general | solution.py:54
  141.1 2.7 %fusion.47 = f32[16,512,128]{2,1,0:T(8,128)} fusion(f32[16,512,128]{2,1,0:T(8,128)} %get-tuple-element.409, s32[]{:T(128)S(6)} %copy.40, f32[2048,128]{1,0:T(8,128)S(1)} %get-tuple-element.418, s32[2048]{0:T(1024)S(1)} %get-tuple-element.416, s32[512]{0:T(512)S(1)} %iota_add_fusion.7), kind=kOutput, calls=%fused_computation.16.clone.1 | convolution fusion | flops 1611661312 | bytes 1320964 | tf_op jit(solution)/shard_map/while/body/eval_jaxpr/dot_general | solution.py:54
  145.0 2.7 %fusion.47 = f32[16,512,128]{2,1,0:T(8,128)} fusion(f32[16,512,128]{2,1,0:T(8,128)} %get-tuple-element.409, s32[]{:T(128)S(6)} %copy.40, f32[2048,128]{1,0:T(8,128)S(1)} %get-tuple-element.418, s32[2048]{0:T(1024)S(1)} %get-tuple-element.416, s32[512]{0:T(512)S(1)} %iota_add_fusion.7), kind=kOutput, calls=%fused_computation.16.clone.1 | convolution fusion | flops 1611661312 | bytes 1320964 | tf_op jit(solution)/shard_map/while/body/eval_jaxpr/dot_general | solution.py:54
  149.0 2.7 %fusion.47 = f32[16,512,128]{2,1,0:T(8,128)} fusion(f32[16,512,128]{2,1,0:T(8,128)} %get-tuple-element.409, s32[]{:T(128)S(6)} %copy.40, f32[2048,128]{1,0:T(8,128)S(1)} %get-tuple-element.418, s32[2048]{0:T(1024)S(1)} %get-tuple-element.416, s32[512]{0:T(512)S(1)} %iota_add_fusion.7), kind=kOutput, calls=%fused_computation.16.clone.1 | convolution fusion | flops 1611661312 | bytes 1320964 | tf_op jit(solution)/shard_map/while/body/eval_jaxpr/dot_general | solution.py:54
  152.9 2.7 %fusion.47 = f32[16,512,128]{2,1,0:T(8,128)} fusion(f32[16,512,128]{2,1,0:T(8,128)} %get-tuple-element.409, s32[]{:T(128)S(6)} %copy.40, f32[2048,128]{1,0:T(8,128)S(1)} %get-tuple-element.418, s32[2048]{0:T(1024)S(1)} %get-tuple-element.416, s32[512]{0:T(512)S(1)} %iota_add_fusion.7), kind=kOutput, calls=%fused_computation.16.clone.1 | convolution fusion | flops 1611661312 | bytes 1320964 | tf_op jit(solution)/shard_map/while/body/eval_jaxpr/dot_general | solution.py:54
  156.8 2.7 %fusion.47 = f32[16,512,128]{2,1,0:T(8,128)} fusion(f32[16,512,128]{2,1,0:T(8,128)} %get-tuple-element.409, s32[]{:T(128)S(6)} %copy.40, f32[2048,128]{1,0:T(8,128)S(1)} %get-tuple-element.418, s32[2048]{0:T(1024)S(1)} %get-tuple-element.416, s32[512]{0:T(512)S(1)} %iota_add_fusion.7), kind=kOutput, calls=%fused_computation.16.clone.1 | convolution fusion | flops 1611661312 | bytes 1320964 | tf_op jit(solution)/shard_map/while/body/eval_jaxpr/dot_general | solution.py:54
  160.7 2.7 %fusion.47 = f32[16,512,128]{2,1,0:T(8,128)} fusion(f32[16,512,128]{2,1,0:T(8,128)} %get-tuple-element.409, s32[]{:T(128)S(6)} %copy.40, f32[2048,128]{1,0:T(8,128)S(1)} %get-tuple-element.418, s32[2048]{0:T(1024)S(1)} %get-tuple-element.416, s32[512]{0:T(512)S(1)} %iota_add_fusion.7), kind=kOutput, calls=%fused_computation.16.clone.1 | convolution fusion | flops 1611661312 | bytes 1320964 | tf_op jit(solution)/shard_map/while/body/eval_jaxpr/dot_general | solution.py:54
  163.4 3.9 %multiply_reduce_fusion = f32[]{:T(128)} fusion(f32[16,512,128]{2,1,0:T(8,128)} %get-tuple-element.131), kind=kLoop, calls=%fused_computation.27 | loop fusion | flops 2097151 | bytes 4194308 | tf_op jit(solution)/shard_map/reduce_sum | solution.py:106
  167.3 7.3 %psum.28 = f32[]{:T(128)} all-reduce(f32[]{:T(128)} %multiply_reduce_fusion), channel_id=1, replica_groups=mesh['dp_0'=4,'dp_1'=4,'dp_2'=2,'mp'=4] {'dp_0'}, use_global_device_ids=true, to_apply=%region_12.13 | all-reduce | flops 1 | bytes 8 | tf_op jit(solution)/shard_map/psum | solution.py:22
  174.6 7.9 %psum.29 = f32[]{:T(128)} all-reduce(f32[]{:T(128)} %psum.28), channel_id=1, replica_groups=mesh['dp_0'=4,'dp_1'=4,'dp_2'=2,'mp'=4] {'dp_1'}, use_global_device_ids=true, to_apply=%region_13.14 | all-reduce | flops 1 | bytes 8 | tf_op jit(solution)/shard_map/psum | solution.py:22
  182.5 6.9 %psum.30 = f32[]{:T(128)} all-reduce(f32[]{:T(128)} %psum.29), channel_id=1, replica_groups=mesh['dp_0'=4,'dp_1'=4,'dp_2'=2,'mp'=4] {'dp_2'}, use_global_device_ids=true, to_apply=%region_14.15 | all-reduce | flops 1 | bytes 8 | tf_op jit(solution)/shard_map/psum | solution.py:22
  189.4 9.1 %psum.31 = f32[]{:T(128)} all-reduce(f32[]{:T(128)} %psum.30), channel_id=1, replica_groups=mesh['dp_0'=4,'dp_1'=4,'dp_2'=2,'mp'=4] {'mp'}, use_global_device_ids=true, to_apply=%region_15.16 | all-reduce | flops 1 | bytes 8 | tf_op jit(solution)/shard_map/psum | solution.py:22
  199.3 2.7 %broadcast_multiply_fusion = f32[16,512,128]{2,1,0:T(8,128)S(1)} fusion(f32[16,512,128]{2,1,0:T(8,128)} %get-tuple-element.131, f32[]{:T(128)S(6)} %div.34), kind=kLoop, calls=%fused_computation.28 | loop fusion | flops 1048576 | bytes 8388612 | tf_op jit(solution)/shard_map/mul | solution.py:110
  204.0 7.3 %multiply_subtract_fusion = (f32[8192,128]{1,0:T(8,128)}, f32[8192,128]{1,0:T(8,128)}, f32[8192,128]{1,0:T(8,128)}) fusion(f32[8192,128]{1,0:T(8,128)S(1)} %copy-done, f32[16,512,128]{2,1,0:T(8,128)S(1)} %broadcast_multiply_fusion, f32[8192,128]{1,0:T(8,128)S(1)} %copy-done.1, f32[8192,128]{1,0:T(8,128)} %param.15), kind=kLoop, calls=%fused_computation.26 | loop fusion | flops 15728640 | bytes 29360128 | tf_op jit(solution)/shard_map/sub | solution.py:115
  (120 shorter events, 65.4 us)
Async XLA Ops:
  79.4 21.3 %all-to-all-start.1 = ((f32[32,64,128]{2,1,0:T(8,128)}), f32[32,64,128]{2,1,0:T(8,128)S(1)}, u32[]{:S(2)}, u32[]{:S(2)}) async-start(f32[32,64,128]{2,1,0:T(8,128)} %bitcast.7), calls=%async_computation.1 | async-start | bytes 2097152 | tf_op jit(solution)/shard_map/all_to_all | solution.py:99
  199.3 3.5 %copy-start = (f32[8192,128]{1,0:T(8,128)S(1)}, f32[8192,128]{1,0:T(8,128)}, u32[]{:S(2)}) copy-start(f32[8192,128]{1,0:T(8,128)} %param.13) | copy-start | bytes 12582916
  199.3 4.7 %copy-start.1 = (f32[8192,128]{1,0:T(8,128)S(1)}, f32[8192,128]{1,0:T(8,128)}, u32[]{:S(2)}) copy-start(f32[8192,128]{1,0:T(8,128)} %param.14) | copy-start | bytes 12582916
where the time goes:
time: 214 us; the launch traced here: 211 us
  matrix products  53 us (25%)
  other arithmetic  48.4 us (23%)
  blocking collectives  47.6 us (22%)
  local copies, waits for them, and re-layouts  25.9 us (12%)
  waiting for transfers between devices  16.9 us (8%)
  loops' own time  13.8 us (6%)
  starting transfers between devices  4.24 us (2%)
    dot_general x16, matrix products, gather_one_block(): jnp.dot(match.astype(jnp.float32), got, precision=lax.Precision.HIGHEST,...  43 us
    psum x4, blocking collectives, by_axis(): shard = lax.psum(shard, axis)  31.2 us
    all_to_all x1, waiting for transfers between devices, body(): lax.all_to_all(sums.reshape(peers, room, width), DP, split_axis=0, concat...  16.9 us
    all_to_all x1, blocking collectives, body(): lax.all_to_all(row_marks, DP, split_axis=0, concat_axis=0, tiled=True)  16.4 us
    add x16, other arithmetic, gather_one_block(): target = start + jnp.arange(step, dtype=jnp.int32)  10.3 us
    dot_general x4, matrix products, pack_one_block(): jnp.dot(match.astype(jnp.bfloat16), values, preferred_element_type=jnp.fl...  10 us
    dynamic_slice x16, local copies, waits for them, and re-layouts, gather_rows(): lax.map(gather_one_block, block_starts(rows_dev, step))  9.31 us
    reduce_or x4, other arithmetic, first_block(): return jnp.logical_not(jnp.any(earlier, axis=1))  7.6 us
  transfers between devices with their start and end apart: 1, of which 1 were waited for; matrix products, arithmetic and copies ran while one was open for 0% of the time, Pallas kernels for 0%

commit v1 on v0

v1 whole, which is shorter than its diff:
```python
import functools

import jax
import jax.numpy as jnp
from jax import lax
from jax.experimental import pallas as pl
from jax.experimental.pallas import tpu as pltpu
from jax.sharding import PartitionSpec as P

beta_first = 0.9
beta_second = 0.999
learn_rate = 0.01
decay_rate = 0.1
adam_eps = 1e-08
first_fix = 0.9999734386
second_fix = 0.0952078529

LANES = 128
ROOM = 64
TILE = 256
FAN = TILE // ROOM
MESH = pl.DeviceIdType.MESH
BIG = 1 << 30


def one_hot(index, base, rows):
    local = index - base
    local = jnp.where(jnp.logical_and(local >= 0, local < rows), local, -1)
    local = local.astype(jnp.float32).astype(jnp.bfloat16)
    shape = (rows, index.shape[1])
    here = lax.broadcasted_iota(jnp.int32, shape, 0).astype(jnp.float32).astype(jnp.bfloat16)
    return jnp.where(here == local, jnp.bfloat16(1), jnp.bfloat16(0))


def rank_tokens(ids_ref, spread_ref, joined_ref, dest_ref, rows_dev):
    blocks = ids_ref.shape[0]
    ids = ids_ref[...]
    columns = ids.T
    lane = lax.broadcasted_iota(jnp.int32, (LANES, LANES), 1)
    place = lax.broadcasted_iota(jnp.int32, (LANES, LANES), 0)
    for i in range(blocks):
        mine = jnp.broadcast_to(columns[:, i : i + 1], (LANES, LANES))
        local = mine & (rows_dev - 1)
        marks = jnp.where(lane == 0, local >> 6, jnp.where(lane == 1, local & 63, 1))
        marks = jnp.where(lane < 3, marks, 0)
        joined_ref[i * LANES : (i + 1) * LANES, LANES:] = marks.astype(jnp.float32).astype(jnp.bfloat16)
        seen = jnp.logical_and(mine == ids[i : i + 1, :], lane < place)
        for j in range(i):
            seen = jnp.logical_or(seen, mine == ids[j : j + 1, :])
        repeat = jnp.max(jnp.where(seen, 1.0, 0.0), axis=1, keepdims=True)
        spread_ref[i * LANES : (i + 1) * LANES, :] = jnp.where(repeat > 0.0, BIG, mine)

    queries = [jnp.broadcast_to(ids[j : j + 1, :], (8, LANES)) for j in range(blocks)]
    queries.append(lax.broadcasted_iota(jnp.int32, (8, LANES), 1) * rows_dev)

    def count(step, sums):
        for u in range(2):
            other = spread_ref[pl.ds(pl.multiple_of(step * 16, 16) + 8 * u, 8), :]
            sums = tuple(s + jnp.where(other < q, 1, 0) for s, q in zip(sums, queries))
        return sums

    zero = jnp.zeros((8, LANES), jnp.int32)
    sums = lax.fori_loop(0, blocks * LANES // 16, count, (zero,) * (blocks + 1))
    below = [jnp.sum(s.astype(jnp.float32), axis=0, keepdims=True).astype(jnp.int32) for s in sums]
    start = jnp.broadcast_to(below[-1], (8, LANES))
    for j in range(blocks):
        owner = ids[j : j + 1, :] // rows_dev
        first = jnp.take_along_axis(start, jnp.broadcast_to(owner, (8, LANES)), axis=1)[0:1, :]
        dest_ref[:, j * LANES : (j + 1) * LANES] = owner * ROOM + below[j] - first


def exchange_kernel(
    n, others, ids_ref, grads_ref, rows_ref, total_ref,
    spread_ref, joined_ref, dest_ref, sums_ref, marks_ref, got_ref, got_marks_ref, split_ref,
    part_ref, parts_ref, plane_ref, planes_ref,
    load_sem, sums_send, sums_recv, marks_send, marks_recv, part_send, part_recv, plane_send, plane_recv,
):
    me = lax.axis_index("dp")
    col = lax.axis_index("mp")
    groups = n // FAN
    rows_dev = rows_ref.shape[0]
    my_group = me // FAN

    barrier = pltpu.get_barrier_semaphore()

    def greet(step, carry):
        pl.semaphore_signal(barrier, inc=1, device_id={"dp": lax.rem(me + step, n)}, device_id_type=MESH)
        return carry

    lax.fori_loop(1, n, greet, 0)
    for step in range(1, others):
        pl.semaphore_signal(barrier, inc=1, device_id={"mp": lax.rem(col + step, others)}, device_id_type=MESH)

    load = pltpu.make_async_copy(grads_ref, joined_ref.at[:, 0:LANES], load_sem)
    load.start()
    rank_tokens(ids_ref, spread_ref, joined_ref, dest_ref, rows_dev)
    load.wait()
    pl.semaphore_wait(barrier, n - 1 + others - 1)

    def sums_copy(peer, source):
        return pltpu.make_async_remote_copy(
            src_ref=sums_ref.at[peer], dst_ref=got_ref.at[source],
            send_sem=sums_send.at[peer], recv_sem=sums_recv.at[source],
            device_id={"dp": peer}, device_id_type=MESH,
        )

    def marks_copy(peer, source):
        return pltpu.make_async_remote_copy(
            src_ref=marks_ref.at[peer // 2], dst_ref=got_marks_ref.at[source],
            send_sem=marks_send.at[peer], recv_sem=marks_recv.at[source],
            device_id={"dp": peer}, device_id_type=MESH,
        )

    def pack(k, carry):
        tile = lax.rem(my_group + k, groups)
        hot = one_hot(dest_ref[...], tile * TILE, TILE)
        out = jnp.dot(hot, joined_ref[...], preferred_element_type=jnp.float32)
        for a in range(FAN):
            sums_ref[FAN * tile + a] = out[a * ROOM : (a + 1) * ROOM, :LANES]
        for h in range(2):
            turned = out[h * LANES : (h + 1) * LANES, LANES:].T
            times = turned[2:3, :]
            row = (turned[0:1, :] * 64.0 + turned[1:2, :]) / jnp.maximum(times, 1.0)
            marks_ref[2 * tile + h] = jnp.where(times > 0.0, jnp.floor(row + 0.5), -1.0)
        for a in range(FAN):
            peer = FAN * tile + a

            @pl.when(peer != me)
            def _():
                marks_copy(peer, me).start()
                sums_copy(peer, me).start()

        return carry

    lax.fori_loop(0, groups, pack, 0)
    got_ref[me] = sums_ref[me]
    got_marks_ref[me] = marks_ref[me // 2]

    half = lax.rem(me, 2)
    lane = lax.broadcasted_iota(jnp.int32, (1, LANES), 1)

    def take(k, first, last):
        group = lax.rem(my_group - k + groups, groups)
        for a in range(FAN):
            source = FAN * group + a

            @pl.when(source != me)
            def _():
                marks_copy(me, source).wait_recv()
                sums_copy(me, source).wait_recv()

        pieces = []
        for h in range(2):
            left = got_marks_ref[FAN * group + 2 * h]
            right = got_marks_ref[FAN * group + 2 * h + 1]
            low = jnp.where(lane < ROOM, left, pltpu.roll(right, ROOM, 1))
            high = jnp.where(lane < ROOM, pltpu.roll(left, ROOM, 1), right)
            pieces.append(jnp.where(half == 0, low, high))
        marks = jnp.concatenate(pieces, axis=1).astype(jnp.int32)
        for a in range(FAN):
            value = got_ref[FAN * group + a]
            big = value.astype(jnp.bfloat16)
            split_ref[a * ROOM : (a + 1) * ROOM, :LANES] = big
            split_ref[a * ROOM : (a + 1) * ROOM, LANES:] = (value - big.astype(jnp.float32)).astype(jnp.bfloat16)

        def spread(step, squares):
            for u in range(2):
                base = pl.multiple_of((step * 2 + u) * TILE, TILE)
                hot = one_hot(marks, base, TILE)
                out = jnp.dot(hot, split_ref[...], preferred_element_type=jnp.float32)
                rows = out[:, :LANES] + out[:, LANES:]
                if not first:
                    rows = rows + rows_ref[pl.ds(base, TILE), :]
                rows_ref[pl.ds(base, TILE), :] = rows
                if last:
                    squares = squares + jnp.sum((rows * rows).reshape(TILE // 8, 8, LANES), axis=0)
            return squares

        return lax.fori_loop(0, rows_dev // TILE // 2, spread, jnp.zeros((8, LANES), jnp.float32))

    take(0, True, False)
    lax.fori_loop(1, groups - 1, lambda k, c: (take(k, False, False), c)[1], 0)
    squares = take(groups - 1, False, True)

    part_ref[...] = jnp.sum(squares, axis=0, keepdims=True)
    parts_ref[me] = part_ref[...]

    def part_copy(peer, source):
        return pltpu.make_async_remote_copy(
            src_ref=part_ref, dst_ref=parts_ref.at[source],
            send_sem=part_send.at[peer], recv_sem=part_recv.at[source],
            device_id={"dp": peer}, device_id_type=MESH,
        )

    def plane_copy(peer, source):
        return pltpu.make_async_remote_copy(
            src_ref=plane_ref, dst_ref=planes_ref.at[source],
            send_sem=plane_send.at[peer], recv_sem=plane_recv.at[source],
            device_id={"mp": peer}, device_id_type=MESH,
        )

    def each_peer(act):
        def one(step, carry):
            act(lax.rem(me + step, n))
            return carry

        lax.fori_loop(1, n, one, 0)

    each_peer(lambda peer: part_copy(peer, me).start())
    each_peer(lambda peer: part_copy(me, peer).wait_recv())
    plane_ref[...] = jnp.sum(parts_ref[...], axis=0)
    planes_ref[col] = plane_ref[...]
    for step in range(1, others):
        plane_copy(lax.rem(col + step, others), col).start()
    for step in range(1, others):
        plane_copy(col, lax.rem(col + step, others)).wait_recv()
    total_ref[...] = jnp.sum(planes_ref[...], axis=0)

    def drain(peer):
        marks_copy(peer, me).wait_send()
        sums_copy(peer, me).wait_send()
        part_copy(peer, me).wait_send()

    each_peer(drain)
    for step in range(1, others):
        plane_copy(lax.rem(col + step, others), col).wait_send()


def update_kernel(limit, total_ref, rows_ref, table_ref, first_ref, second_ref, new_table_ref, new_first_ref, new_second_ref):
    total = jnp.sum(total_ref[...], axis=1, keepdims=True)
    scale = limit / jnp.maximum(jnp.sqrt(total), limit)
    clipped = scale * rows_ref[...]
    first = beta_first * first_ref[...] + (1.0 - beta_first) * clipped
    second = beta_second * second_ref[...] + (1.0 - beta_second) * clipped * clipped
    new_first_ref[...] = first
    new_second_ref[...] = second
    root = second_fix**0.5
    step = (learn_rate * root / first_fix) * first / (jnp.sqrt(second) + adam_eps * root)
    new_table_ref[...] = (1.0 - learn_rate * decay_rate) * table_ref[...] - step


def body(table, first_moment, second_moment, grads, ids):
    n = lax.axis_size("dp")
    others = lax.axis_size("mp")
    rows_dev, width = table.shape
    tok_dev = grads.shape[0]
    slots = n * ROOM
    groups = n // FAN
    dma = pltpu.SemaphoreType.DMA
    rows, total = pl.pallas_call(
        functools.partial(exchange_kernel, n, others),
        out_shape=(
            jax.ShapeDtypeStruct((rows_dev, width), jnp.float32),
            jax.ShapeDtypeStruct((1, LANES), jnp.float32),
        ),
        in_specs=[pl.BlockSpec(memory_space=pltpu.VMEM), pl.BlockSpec(memory_space=pl.ANY)],
        out_specs=(pl.BlockSpec(memory_space=pltpu.VMEM), pl.BlockSpec(memory_space=pltpu.VMEM)),
        scratch_shapes=[
            pltpu.VMEM((tok_dev, LANES), jnp.int32),
            pltpu.VMEM((tok_dev, 2 * LANES), jnp.bfloat16),
            pltpu.VMEM((1, tok_dev), jnp.int32),
            pltpu.VMEM((n, ROOM, width), jnp.float32),
            pltpu.VMEM((n // 2, 1, LANES), jnp.float32),
            pltpu.VMEM((n, ROOM, width), jnp.float32),
            pltpu.VMEM((n, 1, LANES), jnp.float32),
            pltpu.VMEM((TILE, 2 * LANES), jnp.bfloat16),
            pltpu.VMEM((1, LANES), jnp.float32),
            pltpu.VMEM((n, 1, LANES), jnp.float32),
            pltpu.VMEM((1, LANES), jnp.float32),
            pltpu.VMEM((others, 1, LANES), jnp.float32),
            dma,
            dma((n,)),
            dma((n,)),
            dma((n,)),
            dma((n,)),
            dma((n,)),
            dma((n,)),
            dma((others,)),
            dma((others,)),
        ],
        compiler_params=pltpu.CompilerParams(
            collective_id=0, has_side_effects=True, vmem_limit_bytes=24 * 1024 * 1024
        ),
    )(ids.reshape(tok_dev // LANES, LANES), grads)

    limit = float(tok_dev * n * width * others) ** 0.5
    chunk = 512
    block = pl.BlockSpec((chunk, width), lambda i: (i, 0))
    shape = jax.ShapeDtypeStruct((rows_dev, width), jnp.float32)
    return pl.pallas_call(
        functools.partial(update_kernel, limit),
        grid=(rows_dev // chunk,),
        out_shape=(shape, shape, shape),
        in_specs=[pl.BlockSpec((1, LANES), lambda i: (0, 0)), block, block, block, block],
        out_specs=(block, block, block),
        compiler_params=pltpu.CompilerParams(vmem_limit_bytes=16 * 1024 * 1024),
    )(total, rows, table, first_moment, second_moment)


def solution(mesh):
    placed = (P("dp", "mp"), P("dp", "mp"), P("dp", "mp"), P("dp", "mp"), P("dp"))
    return jax.shard_map(
        body,
        mesh=mesh,
        in_specs=placed,
        out_specs=(P("dp", "mp"), P("dp", "mp"), P("dp", "mp")),
        check_vma=False,
    )
```

time: 214 us -> 77.6 us (0.36); the launches traced: 211 us -> 77.2 us
  Pallas kernels: 0 us -> 68.2 us
  matrix products: 53 us -> 0 us
  other arithmetic: 48.4 us -> 0 us
  blocking collectives: 47.6 us -> 0 us
  local copies, waits for them, and re-layouts: 25.9 us -> 8.29 us
  waiting for transfers between devices: 16.9 us -> 0 us
  loops' own time: 13.8 us -> 0 us
  starting transfers between devices: 4.24 us -> 0 us
    pallas_call x0 -> x2, Pallas kernels: none -> 68.2 us  [the longest x1 59.5 us: body(): pl.pallas_call(functools.partial(exchange_kernel, n, others), out_shape=(...]
    dot_general x20 -> x0, matrix products: 53 us -> none  [the longest x16 43 us: gather_one_block(): jnp.dot(match.astype(jnp.float32), got, precision=lax.Precision.HIGHEST,...]
    psum x4 -> x0, blocking collectives: 31.2 us -> none  [by_axis(): shard = lax.psum(shard, axis)]
    dynamic_slice x40 -> x0, local copies, waits for them, and re-layouts: 23.1 us -> none  [the longest x16 9.31 us: gather_rows(): lax.map(gather_one_block, block_starts(rows_dev, step))]
    all_to_all x1 -> x0, waiting for transfers between devices: 16.9 us -> none  [body(): lax.all_to_all(sums.reshape(peers, room, width), DP, split_axis=0, concat...]
    all_to_all x1 -> x0, blocking collectives: 16.4 us -> none  [body(): lax.all_to_all(row_marks, DP, split_axis=0, concat_axis=0, tiled=True)]
    add x24 -> x0, other arithmetic: 15.4 us -> none  [the longest x16 10.3 us: gather_one_block(): target = start + jnp.arange(step, dtype=jnp.int32)]
    another operation x4 -> x0, loops' own time: 13.8 us -> none  [the longest x1 6.83 us: body(): rank = lax.map(rank_block, block_starts(tok_dev, step)).reshape(tok_dev)]
  transfers between devices with their start and end apart: 1 -> 0, of which waited for: 1 -> 0; matrix products, arithmetic and copies ran while one was open for 0% -> 0% of each run, Pallas kernels for 0% -> 0%
where the time goes in v1:
time: 77.6 us; the launch traced here: 77.2 us
  Pallas kernels  68.2 us (88%)
  local copies, waits for them, and re-layouts  8.29 us (11%)
    pallas_call x1, Pallas kernels, body(): pl.pallas_call(functools.partial(exchange_kernel, n, others), out_shape=(...  59.5 us
    pallas_call x1, Pallas kernels, body(): pl.pallas_call(functools.partial(update_kernel, limit), grid=(rows_dev //...  8.7 us
    unnamed x10, local copies, waits for them, and re-layouts  8.29 us

profile of v1, /device:TPU:1, one launch (start us, length us, event | category | flops | bytes accessed | tf_op | source)
XLA Modules:
  0.0 77.2 jit_solution(6380420112879700619)
XLA Ops:
  0.6 0.0 copy-start.3
  0.6 1.0 %copy-done.3 = bf16[2048,128]{1,0:T(8,128)(2,1)S(1)} copy-done((bf16[2048,128]{1,0:T(8,128)(2,1)S(1)}, bf16[2048,128]{1,0:T(8,128)(2,1)}, u32[]{:S(2)}) %copy-start.3) | copy-done | bytes 524312
  1.7 0.0 copy-start.4
  1.7 0.7 copy-done.4
  2.4 59.5 %shard_map.76 = (f32[8192,128]{1,0:T(8,128)S(1)}, f32[1,128]{1,0:T(1,128)S(1)}) custom-call(s32[16,128]{1,0:T(8,128)S(1)} %bitcast.1, bf16[2048,128]{1,0:T(8,128)(2,1)S(1)} %copy-done.3), custom_call_target="tpu_custom_call" | custom-call | tf_op jit(solution)/shard_map/pallas_call | solution.py:250
  61.9 0.0 copy-start
  61.9 2.2 %copy-done = f32[8192,128]{1,0:T(8,128)S(1)} copy-done((f32[8192,128]{1,0:T(8,128)S(1)}, f32[8192,128]{1,0:T(8,128)}, u32[]{:S(2)}) %copy-start) | copy-done | bytes 4194328
  64.1 0.0 copy-start.1
  64.1 2.2 %copy-done.1 = f32[8192,128]{1,0:T(8,128)S(1)} copy-done((f32[8192,128]{1,0:T(8,128)S(1)}, f32[8192,128]{1,0:T(8,128)}, u32[]{:S(2)}) %copy-start.1) | copy-done | bytes 4194328
  66.3 0.0 copy-start.2
  66.3 2.2 %copy-done.2 = f32[8192,128]{1,0:T(8,128)S(1)} copy-done((f32[8192,128]{1,0:T(8,128)S(1)}, f32[8192,128]{1,0:T(8,128)}, u32[]{:S(2)}) %copy-start.2) | copy-done | bytes 4194328
  68.5 8.7 %shard_map.77 = (f32[8192,128]{1,0:T(8,128)}, f32[8192,128]{1,0:T(8,128)}, f32[8192,128]{1,0:T(8,128)}) custom-call(f32[1,128]{1,0:T(1,128)S(1)} %get-tuple-element.5.total_ref, f32[8192,128]{1,0:T(8,128)S(1)} %get-tuple-element.6.rows_ref, f32[8192,128]{1,0:T(8,128)S(1)} %copy-done, f32[8192,128]{1,0:T(8,128)S(1)} %copy-done.1, f32[8192,128]{1,0:T(8,128)S(1)} %copy-done.2), custom_call_target="tpu_custom_call" | custom-call | tf_op jit(solution)/shard_map/pallas_call | solution.py:290
Async XLA Ops:
  0.6 1.0 %copy-start.3 = (bf16[2048,128]{1,0:T(8,128)(2,1)S(1)}, bf16[2048,128]{1,0:T(8,128)(2,1)}, u32[]{:S(2)}) copy-start(bf16[2048,128]{1,0:T(8,128)(2,1)} %grads_ref.1) | copy-start | bytes 1572868
  1.7 0.7 copy-start.4
  61.9 2.2 %copy-start = (f32[8192,128]{1,0:T(8,128)S(1)}, f32[8192,128]{1,0:T(8,128)}, u32[]{:S(2)}) copy-start(f32[8192,128]{1,0:T(8,128)} %table_ref.1) | copy-start | bytes 12582916
  64.1 2.2 %copy-start.1 = (f32[8192,128]{1,0:T(8,128)S(1)}, f32[8192,128]{1,0:T(8,128)}, u32[]{:S(2)}) copy-start(f32[8192,128]{1,0:T(8,128)} %first_ref.1) | copy-start | bytes 12582916
  66.3 2.2 %copy-start.2 = (f32[8192,128]{1,0:T(8,128)S(1)}, f32[8192,128]{1,0:T(8,128)}, u32[]{:S(2)}) copy-start(f32[8192,128]{1,0:T(8,128)} %second_ref.1) | copy-start | bytes 12582916

commit v2 on v1

v2 whole, which is shorter than its diff:
```python
import functools

import jax
import jax.numpy as jnp
from jax import lax
from jax.experimental import pallas as pl
from jax.experimental.pallas import tpu as pltpu
from jax.sharding import PartitionSpec as P

beta_first = 0.9
beta_second = 0.999
learn_rate = 0.01
decay_rate = 0.1
adam_eps = 1e-08
first_fix = 0.9999734386
second_fix = 0.0952078529

LANES = 128
ROOM = 64
TILE = 256
FAN = TILE // ROOM
MESH = pl.DeviceIdType.MESH
BIG = 1 << 30


def one_hot(index, base, rows):
    local = index - base
    local = jnp.where(jnp.logical_and(local >= 0, local < rows), local, -1)
    local = local.astype(jnp.float32).astype(jnp.bfloat16)
    shape = (rows, index.shape[1])
    here = lax.broadcasted_iota(jnp.int32, shape, 0).astype(jnp.float32).astype(jnp.bfloat16)
    return jnp.where(here == local, jnp.bfloat16(1), jnp.bfloat16(0))


def rank_tokens(ids_ref, spread_ref, joined_ref, dest_ref, rows_dev):
    blocks = ids_ref.shape[0]
    ids = ids_ref[...]
    columns = ids.T
    lane = lax.broadcasted_iota(jnp.int32, (LANES, LANES), 1)
    place = lax.broadcasted_iota(jnp.int32, (LANES, LANES), 0)
    shift = jnp.where(lane == 0, 6, 0)
    keep = jnp.where(lane == 0, rows_dev // 64 - 1, jnp.where(lane == 1, 63, 0))
    one = jnp.where(lane == 2, 1, 0)
    later = jnp.where(lane < place, 0.0, 1.0)
    for i in range(blocks):
        mine = jnp.broadcast_to(columns[:, i : i + 1], (LANES, LANES))
        marks = (lax.shift_right_logical(mine, shift) & keep) | one
        joined_ref[i * LANES : (i + 1) * LANES, LANES:] = marks.astype(jnp.float32).astype(jnp.bfloat16)
        alone = jnp.where(mine == ids[i : i + 1, :], later, 1.0)
        for j in range(i):
            alone = jnp.where(mine == ids[j : j + 1, :], 0.0, alone)
        least = jnp.min(alone, axis=1, keepdims=True)
        spread_ref[i * LANES : (i + 1) * LANES, :] = jnp.where(least > 0.0, mine, BIG)

    queries = [jnp.broadcast_to(ids[j : j + 1, :], (8, LANES)) for j in range(blocks)]
    queries.append(lax.broadcasted_iota(jnp.int32, (8, LANES), 1) * rows_dev)
    sums = []
    for part in (queries[:9], queries[9:]):

        def count(step, found, part=part):
            for u in range(8):
                other = spread_ref[pl.ds(pl.multiple_of(step * 64, 64) + 8 * u, 8), :]
                found = tuple(f + lax.shift_right_logical(other - q, 31) for f, q in zip(found, part))
            return found

        zero = jnp.zeros((8, LANES), jnp.int32)
        sums.extend(lax.fori_loop(0, blocks * LANES // 64, count, (zero,) * len(part)))
    below = [jnp.sum(s.astype(jnp.float32), axis=0, keepdims=True).astype(jnp.int32) for s in sums]
    start = jnp.broadcast_to(below[-1], (8, LANES))
    for j in range(blocks):
        owner = ids[j : j + 1, :] // rows_dev
        first = jnp.take_along_axis(start, jnp.broadcast_to(owner, (8, LANES)), axis=1)[0:1, :]
        dest_ref[:, j * LANES : (j + 1) * LANES] = owner * ROOM + below[j] - first


def stages(groups):
    return [groups // 2, groups * 3 // 4, groups - 1, groups]


def exchange_kernel(
    n, others, rows_dev, ids_hbm, grads_ref, all_ref, where_ref, total_ref,
    ids_ref, spread_ref, joined_ref, dest_ref, sums_ref, marks_ref, got_ref, got_marks_ref, split_ref, names_ref, tags_ref,
    part_ref, parts_ref, plane_ref, planes_ref,
    load_sem, ids_sem, sums_send, sums_recv, marks_send, marks_recv, part_send, part_recv, plane_send, plane_recv,
):
    me = lax.axis_index("dp")
    col = lax.axis_index("mp")
    groups = n // FAN
    my_group = me // FAN

    ids_load = pltpu.make_async_copy(ids_hbm, ids_ref, ids_sem)
    ids_load.start()
    load = pltpu.make_async_copy(grads_ref, joined_ref.at[:, 0:LANES], load_sem)
    load.start()
    barrier = pltpu.get_barrier_semaphore()

    def greet(step, carry):
        pl.semaphore_signal(barrier, inc=1, device_id={"dp": lax.rem(me + step, n)}, device_id_type=MESH)
        return carry

    lax.fori_loop(1, n, greet, 0)
    for step in range(1, others):
        pl.semaphore_signal(barrier, inc=1, device_id={"mp": lax.rem(col + step, others)}, device_id_type=MESH)

    ids_load.wait()
    rank_tokens(ids_ref, spread_ref, joined_ref, dest_ref, rows_dev)
    load.wait()
    pl.semaphore_wait(barrier, n - 1 + others - 1)

    def sums_copy(peer, source, place):
        return pltpu.make_async_remote_copy(
            src_ref=sums_ref.at[peer], dst_ref=got_ref.at[place],
            send_sem=sums_send.at[peer], recv_sem=sums_recv.at[place],
            device_id={"dp": peer}, device_id_type=MESH,
        )

    def marks_copy(peer, source, place):
        return pltpu.make_async_remote_copy(
            src_ref=marks_ref.at[peer // 2], dst_ref=got_marks_ref.at[place],
            send_sem=marks_send.at[peer], recv_sem=marks_recv.at[place],
            device_id={"dp": peer}, device_id_type=MESH,
        )

    seat = lax.rem(me, FAN)

    def pack(k, carry):
        tile = lax.rem(my_group + k, groups)
        hot = one_hot(dest_ref[...], tile * TILE, TILE)
        out = jnp.dot(hot, joined_ref[...], preferred_element_type=jnp.float32)
        for a in range(FAN):
            sums_ref[FAN * tile + a] = out[a * ROOM : (a + 1) * ROOM, :LANES]
        for h in range(2):
            turned = out[h * LANES : (h + 1) * LANES, LANES:].T
            times = turned[2:3, :]
            row = (turned[0:1, :] * 64.0 + turned[1:2, :]) / jnp.maximum(times, 1.0)
            marks_ref[2 * tile + h] = jnp.where(times > 0.0, jnp.floor(row + 0.5), -1.0)
        for a in range(FAN):
            peer = FAN * tile + a

            @pl.when(peer != me)
            def _():
                marks_copy(peer, me, FAN * k + seat).start()
                sums_copy(peer, me, FAN * k + seat).start()

        return carry

    lax.fori_loop(0, groups, pack, 0)
    got_ref[seat] = sums_ref[me]
    got_marks_ref[seat] = marks_ref[me // 2]

    half = lax.rem(me, 2)
    low_lane = lax.broadcasted_iota(jnp.int32, (1, LANES), 1) < ROOM

    def arrive(k):
        for a in range(FAN):
            if k == 0:

                @pl.when(a != seat)
                def _():
                    marks_copy(me, me, a).wait_recv()
                    sums_copy(me, me, a).wait_recv()
            else:
                marks_copy(me, me, FAN * k + a).wait_recv()
                sums_copy(me, me, FAN * k + a).wait_recv()
        for h in range(2):
            left = got_marks_ref[FAN * k + 2 * h]
            right = got_marks_ref[FAN * k + 2 * h + 1]
            low = jnp.where(low_lane, left, pltpu.roll(right, ROOM, 1))
            high = jnp.where(low_lane, pltpu.roll(left, ROOM, 1), right)
            row = jnp.where(half == 0, low, high)
            names_ref[:, k * TILE + h * LANES : k * TILE + (h + 1) * LANES] = row
            tags_ref[k * TILE + h * LANES : k * TILE + (h + 1) * LANES, :] = jnp.broadcast_to(row, (LANES, LANES)).T
            where_ref[2 * k + h : 2 * k + h + 1, :] = jnp.where(row < 0.0, float(rows_dev), row).astype(jnp.int32)
        for a in range(FAN):
            value = got_ref[FAN * k + a]
            big = value.astype(jnp.bfloat16)
            at = pl.ds(k * TILE + a * ROOM, ROOM)
            split_ref[at, :LANES] = big
            split_ref[at, LANES:] = (value - big.astype(jnp.float32)).astype(jnp.bfloat16)

    def match(rows, first, last):
        tags = tags_ref[rows, :]
        hot = [
            jnp.where(tags == names_ref[:, c * LANES : (c + 1) * LANES], 1.0, 0.0).astype(jnp.bfloat16)
            for c in range(first * 2, last * 2)
        ]
        hot = jnp.concatenate(hot, axis=1)
        out = jnp.dot(hot, split_ref[first * TILE : last * TILE, :], preferred_element_type=jnp.float32)
        return out[:, :LANES] + out[:, LANES:]

    def tile_rows(i):
        return pl.ds(pl.multiple_of(i * TILE, TILE), TILE)

    def fresh(i, last):
        all_ref[tile_rows(i), :] = match(tile_rows(i), 0, last)

    def more(i, first, last):
        all_ref[tile_rows(i), :] += match(tile_rows(i), first, last)

    def over(low, high, act):
        lax.fori_loop(low, high, lambda i, c: (act(i), c)[1], 0)

    done = 0
    for last in stages(groups):
        for k in range(done, last):
            arrive(k)
        if last < groups - 1:
            if done > 0:
                over(0, done, lambda i: more(i, done, last))
            over(done, last, lambda i: fresh(i, last))
        else:
            for i in range(done):
                more(i, done, last)
            for i in range(done, last):
                fresh(i, last)
        done = last

    squares = jnp.zeros((8, LANES), jnp.float32)
    for k in range(groups):
        for a in range(FAN):
            at = k * TILE + a * ROOM
            both = got_ref[FAN * k + a] * all_ref[at : at + ROOM, :]
            squares = squares + jnp.sum(both.reshape(ROOM // 8, 8, LANES), axis=0)

    part_ref[...] = jnp.sum(squares, axis=0, keepdims=True)
    parts_ref[me] = part_ref[...]

    def part_copy(peer, source):
        return pltpu.make_async_remote_copy(
            src_ref=part_ref, dst_ref=parts_ref.at[source],
            send_sem=part_send.at[peer], recv_sem=part_recv.at[source],
            device_id={"dp": peer}, device_id_type=MESH,
        )

    def plane_copy(peer, source):
        return pltpu.make_async_remote_copy(
            src_ref=plane_ref, dst_ref=planes_ref.at[source],
            send_sem=plane_send.at[peer], recv_sem=plane_recv.at[source],
            device_id={"mp": peer}, device_id_type=MESH,
        )

    def each_peer(act):
        def one(step, carry):
            act(lax.rem(me + step, n))
            return carry

        lax.fori_loop(1, n, one, 0)

    each_peer(lambda peer: part_copy(peer, me).start())
    each_peer(lambda peer: part_copy(me, peer).wait_recv())
    plane_ref[...] = jnp.sum(parts_ref[...], axis=0)
    planes_ref[col] = plane_ref[...]
    for step in range(1, others):
        plane_copy(lax.rem(col + step, others), col).start()
    for step in range(1, others):
        plane_copy(col, lax.rem(col + step, others)).wait_recv()
    total_ref[...] = jnp.sum(planes_ref[...], axis=0)

    def drain(peer):
        marks_copy(peer, me, 0).wait_send()
        sums_copy(peer, me, 0).wait_send()
        part_copy(peer, me).wait_send()

    each_peer(drain)
    for step in range(1, others):
        plane_copy(lax.rem(col + step, others), col).wait_send()


def update_kernel(
    limit, total_ref, where_hbm, all_ref, table_ref, first_ref, second_ref, new_table_hbm, new_first_hbm, new_second_hbm,
    where_ref, rows_ref, new_table_ref, new_first_ref, new_second_ref, where_sem, out_sem,
):
    load = pltpu.make_async_copy(where_hbm, where_ref, where_sem)
    load.start()
    rows_dev = table_ref.shape[0]
    chunk = 512

    def clear(i, carry):
        rows_ref[pl.ds(pl.multiple_of(i * chunk, chunk), chunk), :] = jnp.zeros((chunk, LANES), jnp.float32)
        return carry

    lax.fori_loop(0, rows_dev // chunk, clear, 0)
    total = jnp.sum(total_ref[...], axis=1, keepdims=True)
    scale = limit / jnp.maximum(jnp.sqrt(total), limit)
    load.wait()

    def place(i, carry):
        base = pl.multiple_of(i * LANES, LANES)
        for u in range(LANES):
            rows_ref[pl.ds(where_ref[i, u], 1), :] = all_ref[pl.ds(base + u, 1), :]
        return carry

    lax.fori_loop(0, all_ref.shape[0] // LANES, place, 0)

    def outs(i):
        at = pl.ds(pl.multiple_of(i * chunk, chunk), chunk)
        return [
            pltpu.make_async_copy(ref.at[at, :], hbm.at[at, :], out_sem.at[w, i])
            for w, (ref, hbm) in enumerate(
                [(new_table_ref, new_table_hbm), (new_first_ref, new_first_hbm), (new_second_ref, new_second_hbm)]
            )
        ]

    root = second_fix**0.5

    def update(i, carry):
        at = pl.ds(pl.multiple_of(i * chunk, chunk), chunk)
        clipped = scale * rows_ref[at, :]
        first = beta_first * first_ref[at, :] + (1.0 - beta_first) * clipped
        second = beta_second * second_ref[at, :] + (1.0 - beta_second) * clipped * clipped
        new_first_ref[at, :] = first
        new_second_ref[at, :] = second
        step = (learn_rate * root / first_fix) * first / (second * lax.rsqrt(second) + adam_eps * root)
        new_table_ref[at, :] = (1.0 - learn_rate * decay_rate) * table_ref[at, :] - step
        for copy in outs(i):
            copy.start()
        return carry

    lax.fori_loop(0, rows_dev // chunk, update, 0)

    def finish(i, carry):
        for copy in outs(i):
            copy.wait()
        return carry

    lax.fori_loop(0, rows_dev // chunk, finish, 0)


def body(table, first_moment, second_moment, grads, ids):
    n = lax.axis_size("dp")
    others = lax.axis_size("mp")
    rows_dev, width = table.shape
    tok_dev = grads.shape[0]
    slots = n * ROOM
    dma = pltpu.SemaphoreType.DMA
    vmem = pl.BlockSpec(memory_space=pltpu.VMEM)
    hbm = pl.BlockSpec(memory_space=pltpu.HBM)
    anywhere = pl.BlockSpec(memory_space=pl.ANY)
    sums, where, total = pl.pallas_call(
        functools.partial(exchange_kernel, n, others, rows_dev),
        out_shape=(
            jax.ShapeDtypeStruct((slots, width), jnp.float32),
            jax.ShapeDtypeStruct((slots // LANES, LANES), jnp.int32),
            jax.ShapeDtypeStruct((1, LANES), jnp.float32),
        ),
        in_specs=[hbm, hbm],
        out_specs=(vmem, vmem, vmem),
        scratch_shapes=[
            pltpu.VMEM((tok_dev // LANES, LANES), jnp.int32),
            pltpu.VMEM((tok_dev, LANES), jnp.int32),
            pltpu.VMEM((tok_dev, 2 * LANES), jnp.bfloat16),
            pltpu.VMEM((1, tok_dev), jnp.int32),
            pltpu.VMEM((n, ROOM, width), jnp.float32),
            pltpu.VMEM((n // 2, 1, LANES), jnp.float32),
            pltpu.VMEM((n, ROOM, width), jnp.float32),
            pltpu.VMEM((n, 1, LANES), jnp.float32),
            pltpu.VMEM((slots, 2 * LANES), jnp.bfloat16),
            pltpu.VMEM((1, slots), jnp.float32),
            pltpu.VMEM((slots, LANES), jnp.float32),
            pltpu.VMEM((1, LANES), jnp.float32),
            pltpu.VMEM((n, 1, LANES), jnp.float32),
            pltpu.VMEM((1, LANES), jnp.float32),
            pltpu.VMEM((others, 1, LANES), jnp.float32),
            dma,
            dma,
            dma((n,)),
            dma((n,)),
            dma((n,)),
            dma((n,)),
            dma((n,)),
            dma((n,)),
            dma((others,)),
            dma((others,)),
        ],
        compiler_params=pltpu.CompilerParams(
            collective_id=0, has_side_effects=True, vmem_limit_bytes=20 * 1024 * 1024
        ),
        cost_estimate=pl.CostEstimate(flops=10**11, bytes_accessed=10**8, transcendentals=0),
    )(ids.reshape(tok_dev // LANES, LANES), grads)

    limit = float(tok_dev * n * width * others) ** 0.5
    shape = jax.ShapeDtypeStruct((rows_dev, width), jnp.float32)
    chunks = rows_dev // 512
    return pl.pallas_call(
        functools.partial(update_kernel, limit),
        out_shape=(shape, shape, shape),
        in_specs=[vmem, anywhere, vmem, vmem, vmem, vmem],
        out_specs=(hbm, hbm, hbm),
        scratch_shapes=[
            pltpu.SMEM((slots // LANES, LANES), jnp.int32),
            pltpu.VMEM((rows_dev + 8, width), jnp.float32),
            pltpu.VMEM((rows_dev, width), jnp.float32),
            pltpu.VMEM((rows_dev, width), jnp.float32),
            pltpu.VMEM((rows_dev, width), jnp.float32),
            dma,
            dma((3, chunks)),
        ],
        compiler_params=pltpu.CompilerParams(vmem_limit_bytes=40 * 1024 * 1024),
    )(total, where, sums, table, first_moment, second_moment)


def solution(mesh):
    placed = (P("dp", "mp"), P("dp", "mp"), P("dp", "mp"), P("dp", "mp"), P("dp"))
    return jax.shard_map(
        body,
        mesh=mesh,
        in_specs=placed,
        out_specs=(P("dp", "mp"), P("dp", "mp"), P("dp", "mp")),
        check_vma=False,
    )
```

time: 77.6 us -> 51.2 us (0.66)
  Pallas kernels: 68.2 us -> 48.4 us
  local copies, waits for them, and re-layouts: 8.29 us -> 1.74 us
    pallas_call x2, Pallas kernels: 68.2 us -> 48.4 us  [the longest x1 41 us: body(): pl.pallas_call(functools.partial(exchange_kernel, n, others, rows_dev), o...]
    unnamed x10, local copies, waits for them, and re-layouts: 8.29 us -> 1.74 us
where the time goes in v2:
time: 51.2 us; the launch traced here: 50.8 us
  Pallas kernels  48.4 us (95%)
  local copies, waits for them, and re-layouts  1.74 us (3%)
  between operations  0.67 us (1%)
    pallas_call x1, Pallas kernels, body(): pl.pallas_call(functools.partial(exchange_kernel, n, others, rows_dev), o...  41 us
    pallas_call x1, Pallas kernels, body(): pl.pallas_call(functools.partial(update_kernel, limit), out_shape=(shape,...  7.46 us
    unnamed x10, local copies, waits for them, and re-layouts  1.74 us

profile of v2, /device:TPU:1, one launch (start us, length us, event | category | flops | bytes accessed | tf_op | source)
XLA Modules:
  0.0 50.8 jit_solution(18250904932896680357)
XLA Ops:
  0.6 0.0 copy-start.3
  0.6 1.0 %copy-done.3 = bf16[2048,128]{1,0:T(8,128)(2,1)S(1)} copy-done((bf16[2048,128]{1,0:T(8,128)(2,1)S(1)}, bf16[2048,128]{1,0:T(8,128)(2,1)}, u32[]{:S(2)}) %copy-start.3) | copy-done | bytes 524312
  1.7 0.0 copy-start.4
  1.7 0.7 %copy-done.4 = s32[2048]{0:T(1024)S(1)} copy-done((s32[2048]{0:T(1024)S(1)}, s32[2048]{0:T(1024)}, u32[]{:S(2)}) %copy-start.4) | copy-done | bytes 8216
  2.4 0.0 copy-start
  2.4 0.0 copy-start.1
  2.4 0.0 copy-start.2
  2.4 41.0 %shard_map.76 = (f32[2048,128]{1,0:T(8,128)S(1)}, s32[16,128]{1,0:T(8,128)S(1)}, f32[1,128]{1,0:T(1,128)S(1)}) custom-call(s32[16,128]{1,0:T(8,128)S(1)} %bitcast.1, bf16[2048,128]{1,0:T(8,128)(2,1)S(1)} %copy-done.3), custom_call_target="tpu_custom_call" | custom-call | flops 99999997952 | bytes 100000000 | tf_op jit(solution)/shard_map/pallas_call | solution.py:339
  43.4 0.0 copy-done
  43.4 0.0 copy-done.1
  43.4 0.0 copy-done.2
  43.4 7.5 %shard_map.77 = (f32[8192,128]{1,0:T(8,128)}, f32[8192,128]{1,0:T(8,128)}, f32[8192,128]{1,0:T(8,128)}) custom-call(f32[1,128]{1,0:T(1,128)S(1)} %get-tuple-element.6.total_ref, s32[16,128]{1,0:T(8,128)S(1)} %get-tuple-element.7.where_hbm, f32[2048,128]{1,0:T(8,128)S(1)} %get-tuple-element.8.all_ref, f32[8192,128]{1,0:T(8,128)S(1)} %copy-done, ...), custom_call_target="tpu_custom_call" | custom-call | tf_op jit(solution)/shard_map/pallas_call | solution.py:384
Async XLA Ops:
  0.6 1.0 %copy-start.3 = (bf16[2048,128]{1,0:T(8,128)(2,1)S(1)}, bf16[2048,128]{1,0:T(8,128)(2,1)}, u32[]{:S(2)}) copy-start(bf16[2048,128]{1,0:T(8,128)(2,1)} %grads_ref.1) | copy-start | bytes 1572868
  1.7 0.7 %copy-start.4 = (s32[2048]{0:T(1024)S(1)}, s32[2048]{0:T(1024)}, u32[]{:S(2)}) copy-start(s32[2048]{0:T(1024)} %param.9) | copy-start | bytes 24580
  2.4 41.0 %copy-start = (f32[8192,128]{1,0:T(8,128)S(1)}, f32[8192,128]{1,0:T(8,128)}, u32[]{:S(2)}) copy-start(f32[8192,128]{1,0:T(8,128)} %table_ref.1) | copy-start | bytes 12582916
  2.4 41.0 %copy-start.1 = (f32[8192,128]{1,0:T(8,128)S(1)}, f32[8192,128]{1,0:T(8,128)}, u32[]{:S(2)}) copy-start(f32[8192,128]{1,0:T(8,128)} %first_ref.1) | copy-start | bytes 12582916
  2.4 41.0 %copy-start.2 = (f32[8192,128]{1,0:T(8,128)S(1)}, f32[8192,128]{1,0:T(8,128)}, u32[]{:S(2)}) copy-start(f32[8192,128]{1,0:T(8,128)} %second_ref.1) | copy-start | bytes 12582916

commit v3 on v2

--- a/solution.py
+++ b/solution.py
@@ -21,18 +21,31 @@
 FAN = TILE // ROOM
 MESH = pl.DeviceIdType.MESH
 BIG = 1 << 30
-
-
-def one_hot(index, base, rows):
-    local = index - base
-    local = jnp.where(jnp.logical_and(local >= 0, local < rows), local, -1)
-    local = local.astype(jnp.float32).astype(jnp.bfloat16)
-    shape = (rows, index.shape[1])
-    here = lax.broadcasted_iota(jnp.int32, shape, 0).astype(jnp.float32).astype(jnp.bfloat16)
-    return jnp.where(here == local, jnp.bfloat16(1), jnp.bfloat16(0))
-
-
-def rank_tokens(ids_ref, spread_ref, joined_ref, dest_ref, rows_dev):
+CODES = 32767.0
+
+
+STEPS = [
+    [(0, 0, 0), (0, 0, 1), (2, 2, 0), (2, 2, 1)],
+    [(2, 1, 0), (1, 2, 0), (2, 3, 0), (3, 2, 0)],
+    [(2, 1, 1), (1, 2, 1), (2, 3, 1), (3, 2, 1)],
+    [(2, 0, 0), (0, 2, 0), (2, 0, 1), (0, 2, 1)],
+    [(1, 1, 0), (3, 3, 0), (1, 3, 0), (3, 1, 0)],
+    [(1, 1, 1), (3, 3, 1), (1, 3, 1), (3, 1, 1)],
+    [(1, 0, 0), (3, 0, 0), (0, 1, 0), (0, 3, 0)],
+    [(1, 0, 1), (3, 0, 1), (0, 1, 1), (0, 3, 1)],
+]
+SIDE = 4
+
+
+def peer_of(me, offset):
+    core = lax.rem(me, 2)
+    z = lax.rem(me // 2, SIDE)
+    y = me // (2 * SIDE)
+    core = 1 - core if offset[2] else core
+    return (lax.rem(y + offset[0], SIDE) * SIDE + lax.rem(z + offset[1], SIDE)) * 2 + core
+
+
+def rank_tokens(ids_ref, spread_ref, joined_ref, owner_ref, slot_ref, rows_dev):
     blocks = ids_ref.shape[0]
     ids = ids_ref[...]
     columns = ids.T
@@ -70,7 +83,8 @@
     for j in range(blocks):
         owner = ids[j : j + 1, :] // rows_dev
         first = jnp.take_along_axis(start, jnp.broadcast_to(owner, (8, LANES)), axis=1)[0:1, :]
-        dest_ref[:, j * LANES : (j + 1) * LANES] = owner * ROOM + below[j] - first
+        owner_ref[:, j * LANES : (j + 1) * LANES] = owner
+        slot_ref[:, j * LANES : (j + 1) * LANES] = below[j] - first
 
 
 def stages(groups):
@@ -79,14 +93,14 @@
 
 def exchange_kernel(
     n, others, rows_dev, ids_hbm, grads_ref, all_ref, where_ref, total_ref,
-    ids_ref, spread_ref, joined_ref, dest_ref, sums_ref, marks_ref, got_ref, got_marks_ref, split_ref, names_ref, tags_ref,
+    ids_ref, spread_ref, joined_ref, owner_ref, slot_ref, sums_ref, marks_ref, got_ref, got_marks_ref, split_ref,
+    names_ref, gains_ref, tags_ref, factors_ref,
     part_ref, parts_ref, plane_ref, planes_ref,
     load_sem, ids_sem, sums_send, sums_recv, marks_send, marks_recv, part_send, part_recv, plane_send, plane_recv,
 ):
     me = lax.axis_index("dp")
     col = lax.axis_index("mp")
     groups = n // FAN
-    my_group = me // FAN
 
     ids_load = pltpu.make_async_copy(ids_hbm, ids_ref, ids_sem)
     ids_load.start()
@@ -103,86 +117,88 @@
         pl.semaphore_signal(barrier, inc=1, device_id={"mp": lax.rem(col + step, others)}, device_id_type=MESH)
 
     ids_load.wait()
-    rank_tokens(ids_ref, spread_ref, joined_ref, dest_ref, rows_dev)
+    rank_tokens(ids_ref, spread_ref, joined_ref, owner_ref, slot_ref, rows_dev)
     load.wait()
-    pl.semaphore_wait(barrier, n - 1 + others - 1)
-
-    def sums_copy(peer, source, place):
+
+    def sums_copy(peer, place):
         return pltpu.make_async_remote_copy(
-            src_ref=sums_ref.at[peer], dst_ref=got_ref.at[place],
-            send_sem=sums_send.at[peer], recv_sem=sums_recv.at[place],
+            src_ref=sums_ref.at[place], dst_ref=got_ref.at[place],
+            send_sem=sums_send.at[place], recv_sem=sums_recv.at[place],
             device_id={"dp": peer}, device_id_type=MESH,
         )
 
-    def marks_copy(peer, source, place):
+    def marks_copy(peer, place):
         return pltpu.make_async_remote_copy(
-            src_ref=marks_ref.at[peer // 2], dst_ref=got_marks_ref.at[place],
-            send_sem=marks_send.at[peer], recv_sem=marks_recv.at[place],
+            src_ref=marks_ref.at[place // 2], dst_ref=got_marks_ref.at[place],
+            send_sem=marks_send.at[place], recv_sem=marks_recv.at[place],
             device_id={"dp": peer}, device_id_type=MESH,
         )
 
-    seat = lax.rem(me, FAN)
-
-    def pack(k, carry):
-        tile = lax.rem(my_group + k, groups)
-        hot = one_hot(dest_ref[...], tile * TILE, TILE)
+    tokens = owner_ref.shape[1]
+    here = lax.broadcasted_iota(jnp.int32, (TILE, tokens), 0).astype(jnp.float32).astype(jnp.bfloat16)
+    lane = lax.broadcasted_iota(jnp.int32, (LANES, LANES), 1)
+
+    for k in range(groups):
+        peers = [peer_of(me, offset) for offset in STEPS[k]]
+        owner = owner_ref[...]
+        slot = slot_ref[...]
+        row = jnp.full_like(slot, -1)
+        for a in range(FAN):
+            row = jnp.where(owner == peers[a], slot + a * ROOM, row)
+        row = row.astype(jnp.float32).astype(jnp.bfloat16)
+        hot = jnp.where(here == row, jnp.bfloat16(1), jnp.bfloat16(0))
         out = jnp.dot(hot, joined_ref[...], preferred_element_type=jnp.float32)
+        for h in range(2):
+            value = out[h * LANES : (h + 1) * LANES, :LANES]
+            most = jnp.max(jnp.abs(value), axis=1, keepdims=True)
+            unit = jnp.maximum(most * ((1.0 + 2.0**-7) / CODES), 1e-30).astype(jnp.bfloat16).astype(jnp.float32)
+            code = jnp.clip(jnp.round(value * (1.0 / unit)), -CODES, CODES).astype(jnp.int32).astype(jnp.int16)
+            for a in range(2):
+                sums_ref[FAN * k + 2 * h + a] = code[a * ROOM : (a + 1) * ROOM, :]
+            turned = jnp.where(lane == 3, unit, out[h * LANES : (h + 1) * LANES, LANES:]).T
+            times = turned[2:3, :]
+            name = (turned[0:1, :] * 64.0 + turned[1:2, :]) / jnp.maximum(times, 1.0)
+            marks_ref[2 * k + h, 0:1, :] = jnp.where(times > 0.0, jnp.floor(name + 0.5), -1.0)
+            marks_ref[2 * k + h, 1:2, :] = turned[3:4, :]
+        if k == 0:
+            pl.semaphore_wait(barrier, n - 1 + others - 1)
         for a in range(FAN):
-            sums_ref[FAN * tile + a] = out[a * ROOM : (a + 1) * ROOM, :LANES]
-        for h in range(2):
-            turned = out[h * LANES : (h + 1) * LANES, LANES:].T
-            times = turned[2:3, :]
-            row = (turned[0:1, :] * 64.0 + turned[1:2, :]) / jnp.maximum(times, 1.0)
-            marks_ref[2 * tile + h] = jnp.where(times > 0.0, jnp.floor(row + 0.5), -1.0)
-        for a in range(FAN):
-            peer = FAN * tile + a
-
-            @pl.when(peer != me)
-            def _():
-                marks_copy(peer, me, FAN * k + seat).start()
-                sums_copy(peer, me, FAN * k + seat).start()
-
-        return carry
-
-    lax.fori_loop(0, groups, pack, 0)
-    got_ref[seat] = sums_ref[me]
-    got_marks_ref[seat] = marks_ref[me // 2]
-
-    half = lax.rem(me, 2)
+            if k + a > 0:
+                marks_copy(peers[a], FAN * k + a).start()
+                sums_copy(peers[a], FAN * k + a).start()
+
+    got_ref[0] = sums_ref[0]
+    got_marks_ref[0] = marks_ref[0]
     low_lane = lax.broadcasted_iota(jnp.int32, (1, LANES), 1) < ROOM
 
     def arrive(k):
         for a in range(FAN):
-            if k == 0:
-
-                @pl.when(a != seat)
-                def _():
-                    marks_copy(me, me, a).wait_recv()
-                    sums_copy(me, me, a).wait_recv()
-            else:
-                marks_copy(me, me, FAN * k + a).wait_recv()
-                sums_copy(me, me, FAN * k + a).wait_recv()
+            if k + a > 0:
+                marks_copy(me, FAN * k + a).wait_recv()
+                sums_copy(me, FAN * k + a).wait_recv()
         for h in range(2):
-            left = got_marks_ref[FAN * k + 2 * h]
-            right = got_marks_ref[FAN * k + 2 * h + 1]
-            low = jnp.where(low_lane, left, pltpu.roll(right, ROOM, 1))
-            high = jnp.where(low_lane, pltpu.roll(left, ROOM, 1), right)
-            row = jnp.where(half == 0, low, high)
-            names_ref[:, k * TILE + h * LANES : k * TILE + (h + 1) * LANES] = row
-            tags_ref[k * TILE + h * LANES : k * TILE + (h + 1) * LANES, :] = jnp.broadcast_to(row, (LANES, LANES)).T
-            where_ref[2 * k + h : 2 * k + h + 1, :] = jnp.where(row < 0.0, float(rows_dev), row).astype(jnp.int32)
+            at = slice(k * TILE + h * LANES, k * TILE + (h + 1) * LANES)
+            low = got_marks_ref[FAN * k + 2 * h]
+            high = got_marks_ref[FAN * k + 2 * h + 1]
+            name = jnp.where(low_lane, low[0:1, :], high[0:1, :])
+            unit = jnp.where(low_lane, low[1:2, :], high[1:2, :])
+            names_ref[:, at] = name
+            gains_ref[:, at] = unit
+            tags_ref[at, :] = jnp.broadcast_to(name, (LANES, LANES)).T
+            factors_ref[at, :] = jnp.broadcast_to(unit, (LANES, LANES)).T
+            where_ref[2 * k + h : 2 * k + h + 1, :] = jnp.where(name < 0.0, float(rows_dev), name).astype(jnp.int32)
         for a in range(FAN):
-            value = got_ref[FAN * k + a]
-            big = value.astype(jnp.bfloat16)
-            at = pl.ds(k * TILE + a * ROOM, ROOM)
+            code = got_ref[FAN * k + a].astype(jnp.int32).astype(jnp.float32)
+            big = code.astype(jnp.bfloat16)
+            at = slice(k * TILE + a * ROOM, k * TILE + (a + 1) * ROOM)
             split_ref[at, :LANES] = big
-            split_ref[at, LANES:] = (value - big.astype(jnp.float32)).astype(jnp.bfloat16)
+            split_ref[at, LANES:] = (code - big.astype(jnp.float32)).astype(jnp.bfloat16)
 
     def match(rows, first, last):
         tags = tags_ref[rows, :]
         hot = [
-            jnp.where(tags == names_ref[:, c * LANES : (c + 1) * LANES], 1.0, 0.0).astype(jnp.bfloat16)
-            for c in range(first * 2, last * 2)
+            jnp.where(tags == names_ref[:, at], gains_ref[:, at], 0.0).astype(jnp.bfloat16)
+            for at in [slice(c * LANES, (c + 1) * LANES) for c in range(first * 2, last * 2)]
         ]
         hot = jnp.concatenate(hot, axis=1)
         out = jnp.dot(hot, split_ref[first * TILE : last * TILE, :], preferred_element_type=jnp.float32)
@@ -219,7 +235,8 @@
     for k in range(groups):
         for a in range(FAN):
             at = k * TILE + a * ROOM
-            both = got_ref[FAN * k + a] * all_ref[at : at + ROOM, :]
+            both = got_ref[FAN * k + a].astype(jnp.int32).astype(jnp.float32) * factors_ref[at : at + ROOM, :]
+            both = both * all_ref[at : at + ROOM, :]
             squares = squares + jnp.sum(both.reshape(ROOM // 8, 8, LANES), axis=0)
 
     part_ref[...] = jnp.sum(squares, axis=0, keepdims=True)
@@ -256,12 +273,10 @@
         plane_copy(col, lax.rem(col + step, others)).wait_recv()
     total_ref[...] = jnp.sum(planes_ref[...], axis=0)
 
-    def drain(peer):
-        marks_copy(peer, me, 0).wait_send()
-        sums_copy(peer, me, 0).wait_send()
-        part_copy(peer, me).wait_send()
-
-    each_peer(drain)
+    each_peer(lambda peer: part_copy(peer, me).wait_send())
+    for place in range(1, n):
+        marks_copy(me, place).wait_send()
+        sums_copy(me, place).wait_send()
     for step in range(1, others):
         plane_copy(lax.rem(col + step, others), col).wait_send()
 
@@ -350,12 +365,15 @@
             pltpu.VMEM((tok_dev, LANES), jnp.int32),
             pltpu.VMEM((tok_dev, 2 * LANES), jnp.bfloat16),
             pltpu.VMEM((1, tok_dev), jnp.int32),
-            pltpu.VMEM((n, ROOM, width), jnp.float32),
-            pltpu.VMEM((n // 2, 1, LANES), jnp.float32),
-            pltpu.VMEM((n, ROOM, width), jnp.float32),
-            pltpu.VMEM((n, 1, LANES), jnp.float32),
+            pltpu.VMEM((1, tok_dev), jnp.int32),
+            pltpu.VMEM((n, ROOM, width), jnp.int16),
+            pltpu.VMEM((n // 2, 2, LANES), jnp.float32),
+            pltpu.VMEM((n, ROOM, width), jnp.int16),
+            pltpu.VMEM((n, 2, LANES), jnp.float32),
             pltpu.VMEM((slots, 2 * LANES), jnp.bfloat16),
             pltpu.VMEM((1, slots), jnp.float32),
+            pltpu.VMEM((1, slots), jnp.float32),
+            pltpu.VMEM((slots, LANES), jnp.float32),
             pltpu.VMEM((slots, LANES), jnp.float32),
             pltpu.VMEM((1, LANES), jnp.float32),
             pltpu.VMEM((n, 1, LANES), jnp.float32),

time: 51.2 us -> 43.7 us (0.85)
  Pallas kernels: 48.4 us -> 40.9 us
    pallas_call x1, Pallas kernels: 41 us -> 33.4 us  [body(): pl.pallas_call(functools.partial(exchange_kernel, n, others, rows_dev), o...]
where the time goes in v3:
time: 43.7 us; the launch traced here: 43.3 us
  Pallas kernels  40.9 us (94%)
  local copies, waits for them, and re-layouts  1.74 us (4%)
  between operations  0.67 us (2%)
    pallas_call x1, Pallas kernels, body(): pl.pallas_call(functools.partial(exchange_kernel, n, others, rows_dev), o...  33.4 us
    pallas_call x1, Pallas kernels, body(): pl.pallas_call(functools.partial(update_kernel, limit), out_shape=(shape,...  7.46 us
    unnamed x10, local copies, waits for them, and re-layouts  1.74 us

profile of v3, /device:TPU:1, one launch (start us, length us, event | category | flops | bytes accessed | tf_op | source)
XLA Modules:
  0.0 43.3 jit_solution(4863893006667630609)
XLA Ops:
  0.6 0.0 copy-start.3
  0.6 1.0 %copy-done.3 = bf16[2048,128]{1,0:T(8,128)(2,1)S(1)} copy-done((bf16[2048,128]{1,0:T(8,128)(2,1)S(1)}, bf16[2048,128]{1,0:T(8,128)(2,1)}, u32[]{:S(2)}) %copy-start.3) | copy-done | bytes 524312
  1.7 0.0 copy-start.4
  1.7 0.7 %copy-done.4 = s32[2048]{0:T(1024)S(1)} copy-done((s32[2048]{0:T(1024)S(1)}, s32[2048]{0:T(1024)}, u32[]{:S(2)}) %copy-start.4) | copy-done | bytes 8216
  2.4 0.0 copy-start
  2.4 0.0 copy-start.1
  2.4 0.0 copy-start.2
  2.4 33.4 %shard_map.76 = (f32[2048,128]{1,0:T(8,128)S(1)}, s32[16,128]{1,0:T(8,128)S(1)}, f32[1,128]{1,0:T(1,128)S(1)}) custom-call(s32[16,128]{1,0:T(8,128)S(1)} %bitcast.1, bf16[2048,128]{1,0:T(8,128)(2,1)S(1)} %copy-done.3), custom_call_target="tpu_custom_call" | custom-call | flops 99999997952 | bytes 100000000 | tf_op jit(solution)/shard_map/pallas_call | solution.py:354
  35.8 0.0 copy-done
  35.8 0.0 copy-done.1
  35.8 0.0 copy-done.2
  35.8 7.5 %shard_map.77 = (f32[8192,128]{1,0:T(8,128)}, f32[8192,128]{1,0:T(8,128)}, f32[8192,128]{1,0:T(8,128)}) custom-call(f32[1,128]{1,0:T(1,128)S(1)} %get-tuple-element.6.total_ref, s32[16,128]{1,0:T(8,128)S(1)} %get-tuple-element.7.where_hbm, f32[2048,128]{1,0:T(8,128)S(1)} %get-tuple-element.8.all_ref, f32[8192,128]{1,0:T(8,128)S(1)} %copy-done, ...), custom_call_target="tpu_custom_call" | custom-call | tf_op jit(solution)/shard_map/pallas_call | solution.py:402
Async XLA Ops:
  0.6 1.0 %copy-start.3 = (bf16[2048,128]{1,0:T(8,128)(2,1)S(1)}, bf16[2048,128]{1,0:T(8,128)(2,1)}, u32[]{:S(2)}) copy-start(bf16[2048,128]{1,0:T(8,128)(2,1)} %grads_ref.1) | copy-start | bytes 1572868
  1.7 0.7 %copy-start.4 = (s32[2048]{0:T(1024)S(1)}, s32[2048]{0:T(1024)}, u32[]{:S(2)}) copy-start(s32[2048]{0:T(1024)} %param.9) | copy-start | bytes 24580
  2.4 33.4 %copy-start = (f32[8192,128]{1,0:T(8,128)S(1)}, f32[8192,128]{1,0:T(8,128)}, u32[]{:S(2)}) copy-start(f32[8192,128]{1,0:T(8,128)} %table_ref.1) | copy-start | bytes 12582916
  2.4 33.4 %copy-start.1 = (f32[8192,128]{1,0:T(8,128)S(1)}, f32[8192,128]{1,0:T(8,128)}, u32[]{:S(2)}) copy-start(f32[8192,128]{1,0:T(8,128)} %first_ref.1) | copy-start | bytes 12582916
  2.4 33.5 %copy-start.2 = (f32[8192,128]{1,0:T(8,128)S(1)}, f32[8192,128]{1,0:T(8,128)}, u32[]{:S(2)}) copy-start(f32[8192,128]{1,0:T(8,128)} %second_ref.1) | copy-start | bytes 12582916

commit v4 on v3

--- a/solution.py
+++ b/solution.py
@@ -85,10 +85,6 @@
         first = jnp.take_along_axis(start, jnp.broadcast_to(owner, (8, LANES)), axis=1)[0:1, :]
         owner_ref[:, j * LANES : (j + 1) * LANES] = owner
         slot_ref[:, j * LANES : (j + 1) * LANES] = below[j] - first
-
-
-def stages(groups):
-    return [groups // 2, groups * 3 // 4, groups - 1, groups]
 
 
 def exchange_kernel(
@@ -204,40 +200,20 @@
         out = jnp.dot(hot, split_ref[first * TILE : last * TILE, :], preferred_element_type=jnp.float32)
         return out[:, :LANES] + out[:, LANES:]
 
-    def tile_rows(i):
-        return pl.ds(pl.multiple_of(i * TILE, TILE), TILE)
-
-    def fresh(i, last):
-        all_ref[tile_rows(i), :] = match(tile_rows(i), 0, last)
-
-    def more(i, first, last):
-        all_ref[tile_rows(i), :] += match(tile_rows(i), first, last)
-
-    def over(low, high, act):
-        lax.fori_loop(low, high, lambda i, c: (act(i), c)[1], 0)
-
+    squares = jnp.zeros((8, LANES), jnp.float32)
     done = 0
-    for last in stages(groups):
+    for last in (groups * 5 // 8, groups):
         for k in range(done, last):
             arrive(k)
-        if last < groups - 1:
-            if done > 0:
-                over(0, done, lambda i: more(i, done, last))
-            over(done, last, lambda i: fresh(i, last))
-        else:
-            for i in range(done):
-                more(i, done, last)
-            for i in range(done, last):
-                fresh(i, last)
+        for k in range(done, last):
+            at = slice(k * TILE, (k + 1) * TILE)
+            near = match(at, k, k + 1)
+            far = match(at, 0, k) if k > 0 else jnp.zeros_like(near)
+            all_ref[at, :] = near + far
+            value = got_ref[FAN * k : FAN * (k + 1)].astype(jnp.int32).astype(jnp.float32).reshape(TILE, LANES)
+            both = value * factors_ref[at, :] * (near + 2.0 * far)
+            squares = squares + jnp.sum(both.reshape(TILE // 8, 8, LANES), axis=0)
         done = last
-
-    squares = jnp.zeros((8, LANES), jnp.float32)
-    for k in range(groups):
-        for a in range(FAN):
-            at = k * TILE + a * ROOM
-            both = got_ref[FAN * k + a].astype(jnp.int32).astype(jnp.float32) * factors_ref[at : at + ROOM, :]
-            both = both * all_ref[at : at + ROOM, :]
-            squares = squares + jnp.sum(both.reshape(ROOM // 8, 8, LANES), axis=0)
 
     part_ref[...] = jnp.sum(squares, axis=0, keepdims=True)
     parts_ref[me] = part_ref[...]
@@ -264,6 +240,11 @@
         lax.fori_loop(1, n, one, 0)
 
     each_peer(lambda peer: part_copy(peer, me).start())
+    for k in range(groups - 1):
+        at = slice(k * TILE, (k + 1) * TILE)
+        all_ref[at, :] = all_ref[at, :] + match(at, k + 1, groups)
+    least = jnp.min(where_ref[0 : 2 * groups, :].astype(jnp.float32), axis=0, keepdims=True)
+    where_ref[2 * groups : 2 * groups + 1, :] = jnp.minimum(least, pltpu.roll(least, ROOM, 1)).astype(jnp.int32)
     each_peer(lambda peer: part_copy(me, peer).wait_recv())
     plane_ref[...] = jnp.sum(parts_ref[...], axis=0)
     planes_ref[col] = plane_ref[...]
@@ -299,13 +280,14 @@
     scale = limit / jnp.maximum(jnp.sqrt(total), limit)
     load.wait()
 
-    def place(i, carry):
-        base = pl.multiple_of(i * LANES, LANES)
-        for u in range(LANES):
-            rows_ref[pl.ds(where_ref[i, u], 1), :] = all_ref[pl.ds(base + u, 1), :]
-        return carry
-
-    lax.fori_loop(0, all_ref.shape[0] // LANES, place, 0)
+    halves = all_ref.shape[0] // LANES
+
+    def place(i):
+        for r in range(halves):
+            for h in range(2):
+                row = where_ref[r, i + h * ROOM]
+                rows_ref[pl.ds(row, 1), :] = all_ref[pl.ds(r * LANES + h * ROOM + i, 1), :]
+        return i + 1
 
     def outs(i):
         at = pl.ds(pl.multiple_of(i * chunk, chunk), chunk)
@@ -318,7 +300,11 @@
 
     root = second_fix**0.5
 
-    def update(i, carry):
+    def update(i, placed):
+        end = (i + 1) * chunk
+        placed = lax.while_loop(
+            lambda s: jnp.logical_and(s < ROOM, where_ref[halves, jnp.minimum(s, ROOM - 1)] < end), place, placed
+        )
         at = pl.ds(pl.multiple_of(i * chunk, chunk), chunk)
         clipped = scale * rows_ref[at, :]
         first = beta_first * first_ref[at, :] + (1.0 - beta_first) * clipped
@@ -329,7 +315,7 @@
         new_table_ref[at, :] = (1.0 - learn_rate * decay_rate) * table_ref[at, :] - step
         for copy in outs(i):
             copy.start()
-        return carry
+        return placed
 
     lax.fori_loop(0, rows_dev // chunk, update, 0)
 
@@ -355,7 +341,7 @@
         functools.partial(exchange_kernel, n, others, rows_dev),
         out_shape=(
             jax.ShapeDtypeStruct((slots, width), jnp.float32),
-            jax.ShapeDtypeStruct((slots // LANES, LANES), jnp.int32),
+            jax.ShapeDtypeStruct((slots // LANES + 8, LANES), jnp.int32),
             jax.ShapeDtypeStruct((1, LANES), jnp.float32),
         ),
         in_specs=[hbm, hbm],
@@ -394,7 +380,7 @@
             collective_id=0, has_side_effects=True, vmem_limit_bytes=20 * 1024 * 1024
         ),
         cost_estimate=pl.CostEstimate(flops=10**11, bytes_accessed=10**8, transcendentals=0),
-    )(ids.reshape(tok_dev // LANES, LANES), grads)
+    )(pltpu.with_memory_space_constraint(ids.reshape(tok_dev // LANES, LANES), pltpu.HBM), pltpu.with_memory_space_constraint(grads, pltpu.HBM))
 
     limit = float(tok_dev * n * width * others) ** 0.5
     shape = jax.ShapeDtypeStruct((rows_dev, width), jnp.float32)
@@ -405,7 +391,7 @@
         in_specs=[vmem, anywhere, vmem, vmem, vmem, vmem],
         out_specs=(hbm, hbm, hbm),
         scratch_shapes=[
-            pltpu.SMEM((slots // LANES, LANES), jnp.int32),
+            pltpu.SMEM((slots // LANES + 8, LANES), jnp.int32),
             pltpu.VMEM((rows_dev + 8, width), jnp.float32),
             pltpu.VMEM((rows_dev, width), jnp.float32),
             pltpu.VMEM((rows_dev, width), jnp.float32),

time: 43.7 us -> 40 us (0.915)
  the two profiles are of different devices: /device:TPU:1 before, /device:TPU:24 now
where the time goes in v4:
time: 40 us; the launch traced here: 39.9 us
  Pallas kernels  39.2 us (98%)
  between operations  0.69 us (2%)
    pallas_call x1, Pallas kernels, body(): pl.pallas_call(functools.partial(exchange_kernel, n, others, rows_dev), o...  31 us
    pallas_call x1, Pallas kernels, body(): pl.pallas_call(functools.partial(update_kernel, limit), out_shape=(shape,...  8.14 us

profile of v4, /device:TPU:24, one launch (start us, length us, event | category | flops | bytes accessed | tf_op | source)
XLA Modules:
  0.0 39.9 jit_solution(7652138789090463728)
XLA Ops:
  0.6 0.0 copy-start
  0.6 0.0 copy-start.1
  0.7 0.0 copy-start.2
  0.7 31.0 %shard_map.76 = (f32[2048,128]{1,0:T(8,128)S(1)}, s32[24,128]{1,0:T(8,128)S(1)}, f32[1,128]{1,0:T(1,128)S(1)}) custom-call(s32[16,128]{1,0:T(8,128)} %bitcast.1, bf16[2048,128]{1,0:T(8,128)(2,1)} %grads_ref.1), custom_call_target="tpu_custom_call" | custom-call | flops 99999997952 | bytes 100000000 | tf_op jit(solution)/shard_map/pallas_call | solution.py:340
  31.7 0.0 copy-done
  31.7 0.0 copy-done.1
  31.7 0.0 copy-done.2
  31.7 8.1 %shard_map.77 = (f32[8192,128]{1,0:T(8,128)}, f32[8192,128]{1,0:T(8,128)}, f32[8192,128]{1,0:T(8,128)}) custom-call(f32[1,128]{1,0:T(1,128)S(1)} %get-tuple-element.6.total_ref, s32[24,128]{1,0:T(8,128)S(1)} %get-tuple-element.7.where_hbm, f32[2048,128]{1,0:T(8,128)S(1)} %get-tuple-element.8.all_ref, f32[8192,128]{1,0:T(8,128)S(1)} %copy-done, ...), custom_call_target="tpu_custom_call" | custom-call | tf_op jit(solution)/shard_map/pallas_call | solution.py:388
Async XLA Ops:
  0.6 31.1 %copy-start = (f32[8192,128]{1,0:T(8,128)S(1)}, f32[8192,128]{1,0:T(8,128)}, u32[]{:S(2)}) copy-start(f32[8192,128]{1,0:T(8,128)} %table_ref.1) | copy-start | bytes 12582916
  0.6 31.1 %copy-start.1 = (f32[8192,128]{1,0:T(8,128)S(1)}, f32[8192,128]{1,0:T(8,128)}, u32[]{:S(2)}) copy-start(f32[8192,128]{1,0:T(8,128)} %first_ref.1) | copy-start | bytes 12582916
  0.7 31.1 %copy-start.2 = (f32[8192,128]{1,0:T(8,128)S(1)}, f32[8192,128]{1,0:T(8,128)}, u32[]{:S(2)}) copy-start(f32[8192,128]{1,0:T(8,128)} %second_ref.1) | copy-start | bytes 12582916

commit v5 on v4

--- a/solution.py
+++ b/solution.py
@@ -20,7 +20,6 @@
 TILE = 256
 FAN = TILE // ROOM
 MESH = pl.DeviceIdType.MESH
-BIG = 1 << 30
 CODES = 32767.0
 
 
@@ -45,53 +44,63 @@
     return (lax.rem(y + offset[0], SIDE) * SIDE + lax.rem(z + offset[1], SIDE)) * 2 + core
 
 
-def rank_tokens(ids_ref, spread_ref, joined_ref, owner_ref, slot_ref, rows_dev):
+def name_slots(ids_ref, spread_ref, lead_ref, planes_ref, slots_ref, slot_ids_ref, n, rows_dev):
     blocks = ids_ref.shape[0]
     ids = ids_ref[...]
     columns = ids.T
     lane = lax.broadcasted_iota(jnp.int32, (LANES, LANES), 1)
     place = lax.broadcasted_iota(jnp.int32, (LANES, LANES), 0)
-    shift = jnp.where(lane == 0, 6, 0)
-    keep = jnp.where(lane == 0, rows_dev // 64 - 1, jnp.where(lane == 1, 63, 0))
-    one = jnp.where(lane == 2, 1, 0)
-    later = jnp.where(lane < place, 0.0, 1.0)
+    earlier = jnp.where(place < lane, 0.0, 1.0)
+    group = 8
     for i in range(blocks):
-        mine = jnp.broadcast_to(columns[:, i : i + 1], (LANES, LANES))
-        marks = (lax.shift_right_logical(mine, shift) & keep) | one
-        joined_ref[i * LANES : (i + 1) * LANES, LANES:] = marks.astype(jnp.float32).astype(jnp.bfloat16)
-        alone = jnp.where(mine == ids[i : i + 1, :], later, 1.0)
-        for j in range(i):
-            alone = jnp.where(mine == ids[j : j + 1, :], 0.0, alone)
-        least = jnp.min(alone, axis=1, keepdims=True)
-        spread_ref[i * LANES : (i + 1) * LANES, :] = jnp.where(least > 0.0, mine, BIG)
-
-    queries = [jnp.broadcast_to(ids[j : j + 1, :], (8, LANES)) for j in range(blocks)]
-    queries.append(lax.broadcasted_iota(jnp.int32, (8, LANES), 1) * rows_dev)
-    sums = []
-    for part in (queries[:9], queries[9:]):
-
-        def count(step, found, part=part):
-            for u in range(8):
-                other = spread_ref[pl.ds(pl.multiple_of(step * 64, 64) + 8 * u, 8), :]
-                found = tuple(f + lax.shift_right_logical(other - q, 31) for f, q in zip(found, part))
-            return found
-
-        zero = jnp.zeros((8, LANES), jnp.int32)
-        sums.extend(lax.fori_loop(0, blocks * LANES // 64, count, (zero,) * len(part)))
-    below = [jnp.sum(s.astype(jnp.float32), axis=0, keepdims=True).astype(jnp.int32) for s in sums]
-    start = jnp.broadcast_to(below[-1], (8, LANES))
+        spread_ref[i * LANES : (i + 1) * LANES, :] = jnp.broadcast_to(columns[:, i : i + 1], (LANES, LANES))
+    owners = lax.broadcasted_iota(jnp.int32, (n, LANES), 0)
     for j in range(blocks):
-        owner = ids[j : j + 1, :] // rows_dev
-        first = jnp.take_along_axis(start, jnp.broadcast_to(owner, (8, LANES)), axis=1)[0:1, :]
-        owner_ref[:, j * LANES : (j + 1) * LANES] = owner
-        slot_ref[:, j * LANES : (j + 1) * LANES] = below[j] - first
+        mine = ids[j : j + 1, :]
+        alone = [jnp.ones((group, LANES), jnp.float32)] * 2
+        for v in range(j * LANES // group):
+            other = spread_ref[v * group : (v + 1) * group, :]
+            alone[v % 2] = jnp.where(other == mine, 0.0, alone[v % 2])
+        for v in range(LANES // group):
+            other = spread_ref[j * LANES + v * group : j * LANES + (v + 1) * group, :]
+            seen = jnp.where(other == mine, earlier[v * group : (v + 1) * group, :], 1.0)
+            alone[v % 2] = jnp.minimum(alone[v % 2], seen)
+        lead = jnp.min(jnp.minimum(alone[0], alone[1]), axis=0, keepdims=True)
+        lead = jnp.where(mine // rows_dev == owners, lead, 0.0)
+        at = slice((j // 2) * n, (j // 2 + 1) * n)
+        lead_ref[at, (j % 2) * LANES : (j % 2 + 1) * LANES] = lead.astype(jnp.bfloat16)
+        local = mine & (rows_dev - 1)
+        cols = slice(j * LANES, (j + 1) * LANES)
+        planes_ref[0:n, cols] = (lead * (local >> 6).astype(jnp.float32)).astype(jnp.bfloat16)
+        planes_ref[n : 2 * n, cols] = (lead * (local & 63).astype(jnp.float32)).astype(jnp.bfloat16)
+        planes_ref[2 * n : 3 * n, cols] = lead.astype(jnp.bfloat16)
+
+    wide = lax.broadcasted_iota(jnp.int32, (TILE, TILE), 1)
+    tall = lax.broadcasted_iota(jnp.int32, (TILE, TILE), 0)
+    before = jnp.where(tall < wide, 1.0, 0.0).astype(jnp.bfloat16)
+    lead = lead_ref[...]
+    ahead = jnp.dot(lead, before, preferred_element_type=jnp.float32)
+    lead = lead.astype(jnp.float32)
+    sizes = jnp.sum(lead, axis=1, keepdims=True)
+    carry = jnp.zeros((n, 1), jnp.float32)
+    seats = lax.broadcasted_iota(jnp.int32, (LANES, TILE), 0).astype(jnp.float32)
+    for b in range(blocks // 2):
+        at = slice(b * n, (b + 1) * n)
+        slot = jnp.sum(lead[at, :] * (ahead[at, :] + carry), axis=0, keepdims=True)
+        slots_ref[:, b * TILE : (b + 1) * TILE] = jnp.where(seats == slot, 1.0, 0.0).astype(jnp.bfloat16)
+        carry = carry + sizes[at, :]
+    held = lax.dot_general(
+        planes_ref[...], slots_ref[...], (((1,), (1,)), ((), ())), preferred_element_type=jnp.float32
+    )
+    name = held[0:n, :] * 64.0 + held[n : 2 * n, :]
+    slot_ids_ref[...] = jnp.where(held[2 * n : 3 * n, :] > 0.5, name.astype(jnp.int32) + owners * rows_dev, -1)
 
 
 def exchange_kernel(
     n, others, rows_dev, ids_hbm, grads_ref, all_ref, where_ref, total_ref,
-    ids_ref, spread_ref, joined_ref, owner_ref, slot_ref, sums_ref, marks_ref, got_ref, got_marks_ref, split_ref,
+    ids_ref, spread_ref, loaded_ref, turned_ref, lead_ref, planes_ref, slots_ref, slot_ids_ref, sums_ref, marks_ref, got_ref, got_marks_ref, split_ref,
     names_ref, gains_ref, tags_ref, factors_ref,
-    part_ref, parts_ref, plane_ref, planes_ref,
+    part_ref, parts_ref, plane_ref, across_ref,
     load_sem, ids_sem, sums_send, sums_recv, marks_send, marks_recv, part_send, part_recv, plane_send, plane_recv,
 ):
     me = lax.axis_index("dp")
@@ -100,7 +109,7 @@
 
     ids_load = pltpu.make_async_copy(ids_hbm, ids_ref, ids_sem)
     ids_load.start()
-    load = pltpu.make_async_copy(grads_ref, joined_ref.at[:, 0:LANES], load_sem)
+    load = pltpu.make_async_copy(grads_ref, loaded_ref, load_sem)
     load.start()
     barrier = pltpu.get_barrier_semaphore()
 
@@ -113,8 +122,12 @@
         pl.semaphore_signal(barrier, inc=1, device_id={"mp": lax.rem(col + step, others)}, device_id_type=MESH)
 
     ids_load.wait()
-    rank_tokens(ids_ref, spread_ref, joined_ref, owner_ref, slot_ref, rows_dev)
+    name_slots(ids_ref, spread_ref, lead_ref, planes_ref, slots_ref, slot_ids_ref, n, rows_dev)
     load.wait()
+    tokens = loaded_ref.shape[0]
+    for i in range(tokens // TILE):
+        at = slice(i * TILE, (i + 1) * TILE)
+        turned_ref[:, at] = loaded_ref[at, :].T
 
     def sums_copy(peer, place):
         return pltpu.make_async_remote_copy(
@@ -130,43 +143,46 @@
             device_id={"dp": peer}, device_id_type=MESH,
         )
 
-    tokens = owner_ref.shape[1]
-    here = lax.broadcasted_iota(jnp.int32, (TILE, tokens), 0).astype(jnp.float32).astype(jnp.bfloat16)
-    lane = lax.broadcasted_iota(jnp.int32, (LANES, LANES), 1)
-
-    for k in range(groups):
+    low_lane = lax.broadcasted_iota(jnp.int32, (1, LANES), 1) < ROOM
+
+    def pack(k):
         peers = [peer_of(me, offset) for offset in STEPS[k]]
-        owner = owner_ref[...]
-        slot = slot_ref[...]
-        row = jnp.full_like(slot, -1)
-        for a in range(FAN):
-            row = jnp.where(owner == peers[a], slot + a * ROOM, row)
-        row = row.astype(jnp.float32).astype(jnp.bfloat16)
-        hot = jnp.where(here == row, jnp.bfloat16(1), jnp.bfloat16(0))
-        out = jnp.dot(hot, joined_ref[...], preferred_element_type=jnp.float32)
+        names = []
+        hot = []
         for h in range(2):
-            value = out[h * LANES : (h + 1) * LANES, :LANES]
-            most = jnp.max(jnp.abs(value), axis=1, keepdims=True)
-            unit = jnp.maximum(most * ((1.0 + 2.0**-7) / CODES), 1e-30).astype(jnp.bfloat16).astype(jnp.float32)
-            code = jnp.clip(jnp.round(value * (1.0 / unit)), -CODES, CODES).astype(jnp.int32).astype(jnp.int16)
+            low = slot_ids_ref[pl.ds(peers[2 * h], 1), :]
+            high = slot_ids_ref[pl.ds(peers[2 * h + 1], 1), :]
+            names.append(jnp.where(low_lane, low, pltpu.roll(high, ROOM, 1)))
+            hot.append(jnp.where(spread_ref[...] == names[h], 1.0, 0.0).astype(jnp.bfloat16))
+        out = jnp.dot(turned_ref[...], jnp.concatenate(hot, axis=1), preferred_element_type=jnp.float32)
+        return peers, names, out
+
+    def keep(k, names, out):
+        most = jnp.max(jnp.abs(out), axis=0, keepdims=True)
+        unit = jnp.maximum(most * ((1.0 + 2.0**-7) / CODES), 1e-30).astype(jnp.bfloat16).astype(jnp.float32)
+        code = jnp.clip(jnp.round(out * (1.0 / unit)), -CODES, CODES)
+        for h in range(2):
+            half = code[:, h * LANES : (h + 1) * LANES].T.astype(jnp.int32).astype(jnp.int16)
             for a in range(2):
-                sums_ref[FAN * k + 2 * h + a] = code[a * ROOM : (a + 1) * ROOM, :]
-            turned = jnp.where(lane == 3, unit, out[h * LANES : (h + 1) * LANES, LANES:]).T
-            times = turned[2:3, :]
-            name = (turned[0:1, :] * 64.0 + turned[1:2, :]) / jnp.maximum(times, 1.0)
-            marks_ref[2 * k + h, 0:1, :] = jnp.where(times > 0.0, jnp.floor(name + 0.5), -1.0)
-            marks_ref[2 * k + h, 1:2, :] = turned[3:4, :]
+                sums_ref[FAN * k + 2 * h + a] = half[a * ROOM : (a + 1) * ROOM, :]
+            name = jnp.where(names[h] < 0, -1, names[h] & (rows_dev - 1))
+            marks_ref[2 * k + h, 0:1, :] = name.astype(jnp.float32)
+            marks_ref[2 * k + h, 1:2, :] = unit[:, h * LANES : (h + 1) * LANES]
+
+    for k in range(0, groups, 2):
+        both = [pack(k), pack(k + 1)]
+        for u in range(2):
+            keep(k + u, both[u][1], both[u][2])
         if k == 0:
             pl.semaphore_wait(barrier, n - 1 + others - 1)
-        for a in range(FAN):
-            if k + a > 0:
-                marks_copy(peers[a], FAN * k + a).start()
-                sums_copy(peers[a], FAN * k + a).start()
+        for u in range(2):
+            for a in range(FAN):
+                if k + u + a > 0:
+                    marks_copy(both[u][0][a], FAN * (k + u) + a).start()
+                    sums_copy(both[u][0][a], FAN * (k + u) + a).start()
 
     got_ref[0] = sums_ref[0]
     got_marks_ref[0] = marks_ref[0]
-    low_lane = lax.broadcasted_iota(jnp.int32, (1, LANES), 1) < ROOM
-
     def arrive(k):
         for a in range(FAN):
             if k + a > 0:
@@ -227,7 +243,7 @@
 
     def plane_copy(peer, source):
         return pltpu.make_async_remote_copy(
-            src_ref=plane_ref, dst_ref=planes_ref.at[source],
+            src_ref=plane_ref, dst_ref=across_ref.at[source],
             send_sem=plane_send.at[peer], recv_sem=plane_recv.at[source],
             device_id={"mp": peer}, device_id_type=MESH,
         )
@@ -243,16 +259,14 @@
     for k in range(groups - 1):
         at = slice(k * TILE, (k + 1) * TILE)
         all_ref[at, :] = all_ref[at, :] + match(at, k + 1, groups)
-    least = jnp.min(where_ref[0 : 2 * groups, :].astype(jnp.float32), axis=0, keepdims=True)
-    where_ref[2 * groups : 2 * groups + 1, :] = jnp.minimum(least, pltpu.roll(least, ROOM, 1)).astype(jnp.int32)
     each_peer(lambda peer: part_copy(me, peer).wait_recv())
     plane_ref[...] = jnp.sum(parts_ref[...], axis=0)
-    planes_ref[col] = plane_ref[...]
+    across_ref[col] = plane_ref[...]
     for step in range(1, others):
         plane_copy(lax.rem(col + step, others), col).start()
     for step in range(1, others):
         plane_copy(col, lax.rem(col + step, others)).wait_recv()
-    total_ref[...] = jnp.sum(planes_ref[...], axis=0)
+    total_ref[...] = jnp.sum(across_ref[...], axis=0)
 
     each_peer(lambda peer: part_copy(peer, me).wait_send())
     for place in range(1, n):
@@ -282,12 +296,13 @@
 
     halves = all_ref.shape[0] // LANES
 
-    def place(i):
-        for r in range(halves):
-            for h in range(2):
-                row = where_ref[r, i + h * ROOM]
-                rows_ref[pl.ds(row, 1), :] = all_ref[pl.ds(r * LANES + h * ROOM + i, 1), :]
-        return i + 1
+    def place(i, carry):
+        base = pl.multiple_of(i * LANES, LANES)
+        for u in range(LANES):
+            rows_ref[pl.ds(where_ref[i, u], 1), :] = all_ref[pl.ds(base + u, 1), :]
+        return carry
+
+    lax.fori_loop(0, all_ref.shape[0] // LANES, place, 0)
 
     def outs(i):
         at = pl.ds(pl.multiple_of(i * chunk, chunk), chunk)
@@ -300,11 +315,7 @@
 
     root = second_fix**0.5
 
-    def update(i, placed):
-        end = (i + 1) * chunk
-        placed = lax.while_loop(
-            lambda s: jnp.logical_and(s < ROOM, where_ref[halves, jnp.minimum(s, ROOM - 1)] < end), place, placed
-        )
+    def update(i, carry):
         at = pl.ds(pl.multiple_of(i * chunk, chunk), chunk)
         clipped = scale * rows_ref[at, :]
         first = beta_first * first_ref[at, :] + (1.0 - beta_first) * clipped
@@ -315,7 +326,7 @@
         new_table_ref[at, :] = (1.0 - learn_rate * decay_rate) * table_ref[at, :] - step
         for copy in outs(i):
             copy.start()
-        return placed
+        return carry
 
     lax.fori_loop(0, rows_dev // chunk, update, 0)
 
@@ -341,7 +352,7 @@
         functools.partial(exchange_kernel, n, others, rows_dev),
         out_shape=(
             jax.ShapeDtypeStruct((slots, width), jnp.float32),
-            jax.ShapeDtypeStruct((slots // LANES + 8, LANES), jnp.int32),
+            jax.ShapeDtypeStruct((slots // LANES, LANES), jnp.int32),
             jax.ShapeDtypeStruct((1, LANES), jnp.float32),
         ),
         in_specs=[hbm, hbm],
@@ -349,9 +360,12 @@
         scratch_shapes=[
             pltpu.VMEM((tok_dev // LANES, LANES), jnp.int32),
             pltpu.VMEM((tok_dev, LANES), jnp.int32),
-            pltpu.VMEM((tok_dev, 2 * LANES), jnp.bfloat16),
-            pltpu.VMEM((1, tok_dev), jnp.int32),
-            pltpu.VMEM((1, tok_dev), jnp.int32),
+            pltpu.VMEM((tok_dev, LANES), jnp.bfloat16),
+            pltpu.VMEM((LANES, tok_dev), jnp.bfloat16),
+            pltpu.VMEM((tok_dev // TILE * n, TILE), jnp.bfloat16),
+            pltpu.VMEM((3 * n, tok_dev), jnp.bfloat16),
+            pltpu.VMEM((LANES, tok_dev), jnp.bfloat16),
+            pltpu.VMEM((n, LANES), jnp.int32),
             pltpu.VMEM((n, ROOM, width), jnp.int16),
             pltpu.VMEM((n // 2, 2, LANES), jnp.float32),
             pltpu.VMEM((n, ROOM, width), jnp.int16),
@@ -391,7 +405,7 @@
         in_specs=[vmem, anywhere, vmem, vmem, vmem, vmem],
         out_specs=(hbm, hbm, hbm),
         scratch_shapes=[
-            pltpu.SMEM((slots // LANES + 8, LANES), jnp.int32),
+            pltpu.SMEM((slots // LANES, LANES), jnp.int32),
             pltpu.VMEM((rows_dev + 8, width), jnp.float32),
             pltpu.VMEM((rows_dev, width), jnp.float32),
             pltpu.VMEM((rows_dev, width), jnp.float32),

time: 40 us -> 37.2 us (0.930)
  the two profiles are of different devices: /device:TPU:24 before, /device:TPU:1 now
where the time goes in v5:
time: 37.2 us; the launch traced here: 37 us
  Pallas kernels  36.3 us (98%)
  between operations  0.69 us (2%)
    pallas_call x1, Pallas kernels, body(): pl.pallas_call(functools.partial(exchange_kernel, n, others, rows_dev), o...  28.8 us
    pallas_call x1, Pallas kernels, body(): pl.pallas_call(functools.partial(update_kernel, limit), out_shape=(shape,...  7.46 us

profile of v5, /device:TPU:1, one launch (start us, length us, event | category | flops | bytes accessed | tf_op | source)
XLA Modules:
  0.0 37.0 jit_solution(3797472851312309304)
XLA Ops:
  0.6 0.0 copy-start
  0.6 0.0 copy-start.1
  0.7 0.0 copy-start.2
  0.7 28.8 %shard_map.76 = (f32[2048,128]{1,0:T(8,128)S(1)}, s32[16,128]{1,0:T(8,128)S(1)}, f32[1,128]{1,0:T(1,128)S(1)}) custom-call(s32[16,128]{1,0:T(8,128)} %bitcast.1, bf16[2048,128]{1,0:T(8,128)(2,1)} %grads_ref.1), custom_call_target="tpu_custom_call" | custom-call | flops 99999997952 | bytes 100000000 | tf_op jit(solution)/shard_map/pallas_call | solution.py:351
  29.5 0.0 copy-done
  29.5 0.0 copy-done.1
  29.5 0.0 copy-done.2
  29.5 7.5 %shard_map.77 = (f32[8192,128]{1,0:T(8,128)}, f32[8192,128]{1,0:T(8,128)}, f32[8192,128]{1,0:T(8,128)}) custom-call(f32[1,128]{1,0:T(1,128)S(1)} %get-tuple-element.6.total_ref, s32[16,128]{1,0:T(8,128)S(1)} %get-tuple-element.7.where_hbm, f32[2048,128]{1,0:T(8,128)S(1)} %get-tuple-element.8.all_ref, f32[8192,128]{1,0:T(8,128)S(1)} %copy-done, ...), custom_call_target="tpu_custom_call" | custom-call | tf_op jit(solution)/shard_map/pallas_call | solution.py:402
Async XLA Ops:
  0.6 28.8 %copy-start = (f32[8192,128]{1,0:T(8,128)S(1)}, f32[8192,128]{1,0:T(8,128)}, u32[]{:S(2)}) copy-start(f32[8192,128]{1,0:T(8,128)} %table_ref.1) | copy-start | bytes 12582916
  0.6 28.8 %copy-start.1 = (f32[8192,128]{1,0:T(8,128)S(1)}, f32[8192,128]{1,0:T(8,128)}, u32[]{:S(2)}) copy-start(f32[8192,128]{1,0:T(8,128)} %first_ref.1) | copy-start | bytes 12582916
  0.7 28.8 %copy-start.2 = (f32[8192,128]{1,0:T(8,128)S(1)}, f32[8192,128]{1,0:T(8,128)}, u32[]{:S(2)}) copy-start(f32[8192,128]{1,0:T(8,128)} %second_ref.1) | copy-start | bytes 12582916

commit v6 on v5

--- a/solution.py
+++ b/solution.py
@@ -34,6 +34,12 @@
     [(1, 0, 1), (3, 0, 1), (0, 1, 1), (0, 3, 1)],
 ]
 SIDE = 4
+
+
+def far_first():
+    hops = [0, 1, 2, 1]
+    away = [offset for step in STEPS for offset in step if any(offset)]
+    return sorted(away, key=lambda offset: -(hops[offset[0]] + hops[offset[1]]))
 
 
 def peer_of(me, offset):
@@ -93,7 +99,18 @@
         planes_ref[...], slots_ref[...], (((1,), (1,)), ((), ())), preferred_element_type=jnp.float32
     )
     name = held[0:n, :] * 64.0 + held[n : 2 * n, :]
-    slot_ids_ref[...] = jnp.where(held[2 * n : 3 * n, :] > 0.5, name.astype(jnp.int32) + owners * rows_dev, -1)
+    name = jnp.where(held[2 * n : 3 * n, :] > 0.5, name, float(rows_dev)).astype(jnp.int32)
+    seat = lax.broadcasted_iota(jnp.int32, (n, LANES), 1)
+    name = jnp.where(seat < ROOM, name, pltpu.roll(name, ROOM, 1))
+    rank = jnp.zeros((n, LANES), jnp.int32)
+    for r in range(1, ROOM):
+        rank = rank + lax.shift_right_logical(pltpu.roll(name, r, 1) - name, 31)
+    both = name * ROOM + rank
+    ordered = jnp.where(rank == seat, name, rows_dev)
+    for r in range(1, ROOM):
+        moved = pltpu.roll(both, r, 1)
+        ordered = jnp.where((moved & (ROOM - 1)) == seat, moved >> 6, ordered)
+    slot_ids_ref[...] = jnp.where(ordered < rows_dev, ordered + owners * rows_dev, -1)
 
 
 def exchange_kernel(
@@ -218,7 +235,7 @@
 
     squares = jnp.zeros((8, LANES), jnp.float32)
     done = 0
-    for last in (groups * 5 // 8, groups):
+    for last in (groups // 2, groups * 3 // 4, groups):
         for k in range(done, last):
             arrive(k)
         for k in range(done, last):
@@ -255,10 +272,13 @@
 
         lax.fori_loop(1, n, one, 0)
 
-    each_peer(lambda peer: part_copy(peer, me).start())
+    for offset in far_first():
+        part_copy(peer_of(me, offset), me).start()
     for k in range(groups - 1):
         at = slice(k * TILE, (k + 1) * TILE)
         all_ref[at, :] = all_ref[at, :] + match(at, k + 1, groups)
+    least = jnp.min(where_ref[0 : 2 * groups, :].astype(jnp.float32), axis=0, keepdims=True)
+    where_ref[2 * groups : 2 * groups + 1, :] = jnp.minimum(least, pltpu.roll(least, ROOM, 1)).astype(jnp.int32)
     each_peer(lambda peer: part_copy(me, peer).wait_recv())
     plane_ref[...] = jnp.sum(parts_ref[...], axis=0)
     across_ref[col] = plane_ref[...]
@@ -296,13 +316,16 @@
 
     halves = all_ref.shape[0] // LANES
 
-    def place(i, carry):
-        base = pl.multiple_of(i * LANES, LANES)
-        for u in range(LANES):
-            rows_ref[pl.ds(where_ref[i, u], 1), :] = all_ref[pl.ds(base + u, 1), :]
-        return carry
-
-    lax.fori_loop(0, all_ref.shape[0] // LANES, place, 0)
+    halves = all_ref.shape[0] // LANES
+    burst = 4
+
+    def place(i):
+        for r in range(halves):
+            for h in range(2):
+                for u in range(burst):
+                    row = where_ref[i + (r * LANES + h * ROOM + u)]
+                    rows_ref[pl.ds(row, 1), :] = all_ref[pl.ds(i + (r * LANES + h * ROOM + u), 1), :]
+        return i + burst
 
     def outs(i):
         at = pl.ds(pl.multiple_of(i * chunk, chunk), chunk)
@@ -313,20 +336,26 @@
             )
         ]
 
+    first_gain = (1.0 - beta_first) * scale
+    second_gain = (1.0 - beta_second) * scale * scale
     root = second_fix**0.5
 
-    def update(i, carry):
+    def update(i, placed):
+        end = (i + 1) * chunk
+        placed = lax.while_loop(
+            lambda s: jnp.logical_and(s < ROOM, where_ref[halves * LANES + jnp.minimum(s, ROOM - 1)] < end), place, placed
+        )
         at = pl.ds(pl.multiple_of(i * chunk, chunk), chunk)
-        clipped = scale * rows_ref[at, :]
-        first = beta_first * first_ref[at, :] + (1.0 - beta_first) * clipped
-        second = beta_second * second_ref[at, :] + (1.0 - beta_second) * clipped * clipped
+        grad = rows_ref[at, :]
+        first = beta_first * first_ref[at, :] + first_gain * grad
+        second = beta_second * second_ref[at, :] + second_gain * (grad * grad)
         new_first_ref[at, :] = first
         new_second_ref[at, :] = second
         step = (learn_rate * root / first_fix) * first / (second * lax.rsqrt(second) + adam_eps * root)
         new_table_ref[at, :] = (1.0 - learn_rate * decay_rate) * table_ref[at, :] - step
         for copy in outs(i):
             copy.start()
-        return carry
+        return placed
 
     lax.fori_loop(0, rows_dev // chunk, update, 0)
 
@@ -352,7 +381,7 @@
         functools.partial(exchange_kernel, n, others, rows_dev),
         out_shape=(
             jax.ShapeDtypeStruct((slots, width), jnp.float32),
-            jax.ShapeDtypeStruct((slots // LANES, LANES), jnp.int32),
+            jax.ShapeDtypeStruct((slots // LANES + 8, LANES), jnp.int32),
             jax.ShapeDtypeStruct((1, LANES), jnp.float32),
         ),
         in_specs=[hbm, hbm],
@@ -405,7 +434,7 @@
         in_specs=[vmem, anywhere, vmem, vmem, vmem, vmem],
         out_specs=(hbm, hbm, hbm),
         scratch_shapes=[
-            pltpu.SMEM((slots // LANES, LANES), jnp.int32),
+            pltpu.SMEM((slots + 8 * LANES,), jnp.int32),
             pltpu.VMEM((rows_dev + 8, width), jnp.float32),
             pltpu.VMEM((rows_dev, width), jnp.float32),
             pltpu.VMEM((rows_dev, width), jnp.float32),
@@ -414,7 +443,7 @@
             dma((3, chunks)),
         ],
         compiler_params=pltpu.CompilerParams(vmem_limit_bytes=40 * 1024 * 1024),
-    )(total, where, sums, table, first_moment, second_moment)
+    )(total, where.reshape(slots + 8 * LANES), sums, table, first_moment, second_moment)
 
 
 def solution(mesh):

time: 37.2 us -> 35.9 us (0.965)
  Pallas kernels: 36.3 us -> 34.7 us
    pallas_call x1, Pallas kernels: 7.46 us -> 5.96 us  [body(): pl.pallas_call(functools.partial(update_kernel, limit), out_shape=(shape,...]
where the time goes in v6:
time: 35.9 us; the launch traced here: 35.4 us
  Pallas kernels  34.7 us (97%)
  between operations  0.69 us (2%)
    pallas_call x1, Pallas kernels, body(): pl.pallas_call(functools.partial(exchange_kernel, n, others, rows_dev), o...  28.8 us
    pallas_call x1, Pallas kernels, body(): pl.pallas_call(functools.partial(update_kernel, limit), out_shape=(shape,...  5.96 us

profile of v6, /device:TPU:1, one launch (start us, length us, event | category | flops | bytes accessed | tf_op | source)
XLA Modules:
  0.0 35.4 jit_solution(5996875876224853230)
XLA Ops:
  0.6 0.0 copy-start
  0.6 0.0 copy-start.1
  0.7 0.0 copy-start.2
  0.7 28.8 %shard_map.76 = (f32[2048,128]{1,0:T(8,128)S(1)}, s32[24,128]{1,0:T(8,128)S(1)}, f32[1,128]{1,0:T(1,128)S(1)}) custom-call(s32[16,128]{1,0:T(8,128)} %bitcast.3, bf16[2048,128]{1,0:T(8,128)(2,1)} %grads_ref.1), custom_call_target="tpu_custom_call" | custom-call | flops 99999997952 | bytes 100000000 | tf_op jit(solution)/shard_map/pallas_call | solution.py:380
  29.5 0.0 copy-done
  29.5 0.0 copy-done.1
  29.5 0.0 copy-done.2
  29.5 6.0 %shard_map.77 = (f32[8192,128]{1,0:T(8,128)}, f32[8192,128]{1,0:T(8,128)}, f32[8192,128]{1,0:T(8,128)}) custom-call(f32[1,128]{1,0:T(1,128)S(1)} %get-tuple-element.6.total_ref, s32[3072]{0:T(1024)S(1)} %bitcast.2, f32[2048,128]{1,0:T(8,128)S(1)} %get-tuple-element.8.all_ref, f32[8192,128]{1,0:T(8,128)S(1)} %copy-done, f32[8192,128]{1,0:T(8,128)S(1)} %copy-done.1, ...), custom_call_target="tpu_custom_call" | custom-call | tf_op jit(solution)/shard_map/pallas_call | solution.py:431
Async XLA Ops:
  0.6 28.8 %copy-start = (f32[8192,128]{1,0:T(8,128)S(1)}, f32[8192,128]{1,0:T(8,128)}, u32[]{:S(2)}) copy-start(f32[8192,128]{1,0:T(8,128)} %table_ref.1) | copy-start | bytes 12582916
  0.6 28.8 %copy-start.1 = (f32[8192,128]{1,0:T(8,128)S(1)}, f32[8192,128]{1,0:T(8,128)}, u32[]{:S(2)}) copy-start(f32[8192,128]{1,0:T(8,128)} %first_ref.1) | copy-start | bytes 12582916
  0.7 28.8 %copy-start.2 = (f32[8192,128]{1,0:T(8,128)S(1)}, f32[8192,128]{1,0:T(8,128)}, u32[]{:S(2)}) copy-start(f32[8192,128]{1,0:T(8,128)} %second_ref.1) | copy-start | bytes 12582916
